TPU v7x, 32 devices: a whole 2x2x4 slice. The times are simulated.
32 devices in a mesh: dp: 2 (over x), row: 4 (over y, core), col: 4 (over z).
Axes of the slice: x: 2, y: 2, z: 4, core: 2. Of those that a mesh axis runs over, the one named last changes fastest.
Arguments:
- hidden_in: bfloat16 [2048, 2048], P(('dp', 'row'), 'col'), may hold values from -6 to 6
- cotangent: bfloat16 [2048, 2048], P(('dp', 'row'), 'col'), may hold values from -6 to 6
- segment_ids: int32 [8, 256], P(('dp', 'col')), may hold values from 0 to 3, never falling along the last dimension, each value on 1 to 128 neighbouring positions
- w_qkv: bfloat16 [2048, 3, 2048], P('col', None, 'row'), may hold values from -0.125 to 0.125
- b_qkv: bfloat16 [3, 2048], P(None, 'row'), may hold values from -6 to 6
- w_fc1: bfloat16 [2048, 8192], P('col', 'row'), may hold values from -0.125 to 0.125
- b_fc1: bfloat16 [8192], P('row'), may hold values from -3 to 3
- w_dense: bfloat16 [2048, 2048], P('row', 'col'), may hold values from -1 to 1
- w_fc2: bfloat16 [8192, 2048], P('row', 'col'), may hold values from -0.0625 to 0.0625
- out_bias: bfloat16 [2048], P('col'), may hold values from -3 to 3
- ln_gain: bfloat16 [2048], P('col'), may hold values from 0.099609375 to 1.8984375
- ln_shift: bfloat16 [2048], P('col'), may hold values from -2 to 2
Outputs:
- output: bfloat16 [2048, 2048], P(('dp', 'row'), 'col')
- grad_input: float32 [2048, 2048], P(('dp', 'row'), 'col')
- grad_w_qkv: float32 [2048, 3, 2048], P('col', None, 'row')
- grad_b_qkv: float32 [3, 2048], P(None, 'row')
- grad_w_fc1: float32 [2048, 8192], P('col', 'row')
- grad_b_fc1: float32 [8192], P('row')
- grad_w_dense: float32 [2048, 2048], P('row', 'col')
- grad_w_fc2: float32 [8192, 2048], P('row', 'col')
- grad_out_bias: float32 [2048], P('col')
- grad_ln_gain: float32 [2048], P('col')
- grad_ln_shift: float32 [2048], P('col')
Inputs may be any that keep to these rules, and one draw needn't show every extreme that they name: `segment_ids`: segment ids never fall along a packed row; each id 0 to 3 covers 1 to 128 consecutive tokens of the row.
All inputs are finite; a program needn't handle non-finite values.
Results may differ from a plain program's by a relative error of at most 0.004.
The roundings to bfloat16 on the way count: a program that leaves them out, or rounds other values in their place, can miss the bound.
Values may be sent and summed in bfloat16 or wider, within the bound.
A program may use at most 256 MiB of HBM per device.

v0:
```python
import jax
import jax.numpy as jnp
from jax import lax
from jax.sharding import PartitionSpec as P

D = 2048
HEAD_DIM = 64
ROT = 32


epsilon = 1e-05
masked_score = -1e30


def rotary_tables(segments):
    length = segments.shape[0]
    position = jnp.arange(length, dtype=jnp.int32)
    boundary = jnp.concatenate([jnp.ones((1,), dtype=bool), segments[1:] != segments[:-1]])
    segment_start = lax.cummax(jnp.where(boundary, position, 0), axis=0)
    offset = (position - segment_start).astype(jnp.float32)
    half_width = ROT // 2
    inverse = 10000.0 ** (-(2.0 * jnp.arange(half_width, dtype=jnp.float32)) / ROT)
    angles = offset[:, None] * inverse[None, :]
    return (jnp.cos(angles)[:, None, :], jnp.sin(angles)[:, None, :])


def rotate(tensor, cosine, sine):
    half_width = ROT // 2
    leading = tensor[..., :half_width]
    trailing = tensor[..., half_width:ROT]
    return jnp.concatenate(
        [leading * cosine - trailing * sine, trailing * cosine + leading * sine, tensor[..., ROT:]],
        axis=-1,
    )


def shards(
    hidden_in,
    cotangent,
    segment_ids,
    w_qkv,
    b_qkv,
    w_fc1,
    b_fc1,
    w_dense,
    w_fc2,
    out_bias,
    ln_gain,
    ln_shift,
):
    seq_len = segment_ids.shape[1]
    local_x = hidden_in.astype(jnp.float32)
    row_sums = lax.psum((jnp.sum(local_x, axis=1), jnp.sum(local_x * local_x, axis=1)), "col")
    row_mean = row_sums[0] / D
    variance = row_sums[1] / D - row_mean * row_mean
    inv_std = lax.rsqrt(variance + epsilon)[:, None]
    centred = (local_x - row_mean[:, None]) * inv_std
    gain_f = ln_gain.astype(jnp.float32)
    normed = (centred * gain_f + ln_shift.astype(jnp.float32)).astype(jnp.bfloat16)
    normed_all = lax.all_gather(normed, "row", axis=0, tiled=True)
    grad_rows = lax.all_gather(cotangent, "row", axis=0, tiled=True)
    attn_width = w_qkv.shape[1] * w_qkv.shape[2]
    w_attn = w_qkv.reshape(w_qkv.shape[0], attn_width)
    w_joint = jnp.concatenate([w_attn, w_fc1], axis=1)
    bias_joint = jnp.concatenate([b_qkv.reshape(attn_width), b_fc1]).astype(jnp.float32)
    w_out = jnp.concatenate([w_dense, w_fc2], axis=0)
    row_block = normed_all
    attn_part = lax.psum_scatter(
        jnp.dot(row_block, w_attn, preferred_element_type=jnp.float32),
        "col",
        scatter_dimension=0,
        tiled=True,
    )
    row_block = normed_all
    mlp_part = lax.psum_scatter(
        jnp.dot(row_block, w_fc1, preferred_element_type=jnp.float32),
        "col",
        scatter_dimension=0,
        tiled=True,
    )
    projected = jnp.concatenate([attn_part, mlp_part], axis=1) + bias_joint
    heads_here = w_qkv.shape[2] // HEAD_DIM
    mixed_width = heads_here * HEAD_DIM
    attn_pre = projected[:, :attn_width].reshape(seq_len, 3, heads_here, HEAD_DIM)
    hidden_pre = projected[:, attn_width:]
    segments = segment_ids[0]
    cosine, sine = rotary_tables(segments)
    position = jnp.arange(seq_len, dtype=jnp.int32)
    allowed = (segments[:, None] == segments[None, :]) & (position[:, None] >= position[None, :])
    score_scale = HEAD_DIM ** (-0.5)
    queries = jnp.transpose(rotate(attn_pre[:, 0], cosine, sine).astype(jnp.bfloat16), (1, 0, 2))
    key_heads = jnp.transpose(rotate(attn_pre[:, 1], cosine, sine).astype(jnp.bfloat16), (1, 0, 2))
    values = jnp.transpose(attn_pre[:, 2].astype(jnp.bfloat16), (1, 0, 2))

    def score_block(query_head, key_head):
        scores = (
            jnp.einsum("qd,kd->qk", query_head, key_head, preferred_element_type=jnp.float32)
            * score_scale
        )
        return jnp.where(allowed, scores, masked_score)

    def forward_head(head_item):
        query_head, key_head, value_head = head_item
        scores = score_block(query_head, key_head)
        peak_score = jnp.max(scores, axis=1, keepdims=True)
        exponentials = jnp.exp(scores - peak_score)
        row_total = jnp.sum(exponentials, axis=1, keepdims=True)
        probabilities = (exponentials / row_total).astype(jnp.bfloat16)
        head_out = jnp.dot(probabilities, value_head, preferred_element_type=jnp.float32)
        return (head_out, (peak_score + jnp.log(row_total))[:, 0])

    head_outs, log_totals = lax.map(forward_head, (queries, key_heads, values))
    attn_mixed = (
        jnp.transpose(head_outs, (1, 0, 2)).reshape(seq_len, mixed_width).astype(jnp.bfloat16)
    )
    activated = jax.nn.gelu(hidden_pre, approximate=True).astype(jnp.bfloat16)
    branch_in = jnp.concatenate([attn_mixed, activated], axis=1)
    partial_value = jnp.dot(
        lax.all_gather(branch_in, "col", axis=0, tiled=True),
        w_out,
        preferred_element_type=jnp.float32,
    )
    branch = lax.psum_scatter(partial_value, "row", scatter_dimension=0, tiled=True)
    output = (local_x + branch + out_bias.astype(jnp.float32)).astype(jnp.bfloat16)
    row_block = grad_rows
    grad_branch = lax.psum_scatter(
        jnp.einsum("tc,fc->tf", row_block, w_out, preferred_element_type=jnp.float32),
        "col",
        scatter_dimension=0,
        tiled=True,
    ).astype(jnp.bfloat16)
    row_block = grad_rows
    grad_w_out = jnp.einsum(
        "tf,tc->fc",
        lax.all_gather(branch_in, "col", axis=0, tiled=True),
        row_block,
        preferred_element_type=jnp.float32,
    )
    grad_mixed = jnp.transpose(
        grad_branch[:, :mixed_width].reshape(seq_len, heads_here, HEAD_DIM), (1, 0, 2)
    )
    _, gelu_pull = jax.vjp(lambda pre_values: jax.nn.gelu(pre_values, approximate=True), hidden_pre)
    grad_hidden = gelu_pull(grad_branch[:, mixed_width:].astype(jnp.float32))[0].astype(
        jnp.bfloat16
    )

    def backward_head(head_item):
        query_head, key_head, value_head, log_head, grad_head = head_item
        scores = score_block(query_head, key_head)
        probabilities = jnp.exp(scores - log_head[:, None])
        grad_probs = jnp.einsum(
            "qd,kd->qk", grad_head, value_head, preferred_element_type=jnp.float32
        )
        centre_term = jnp.sum(probabilities * grad_probs, axis=1, keepdims=True)
        grad_scores = (probabilities * (grad_probs - centre_term)).astype(jnp.bfloat16)
        grad_query = (
            jnp.dot(grad_scores, key_head, preferred_element_type=jnp.float32) * score_scale
        )
        grad_key = (
            jnp.einsum("qk,qd->kd", grad_scores, query_head, preferred_element_type=jnp.float32)
            * score_scale
        )
        grad_value = jnp.einsum(
            "qk,qd->kd",
            probabilities.astype(jnp.bfloat16),
            grad_head,
            preferred_element_type=jnp.float32,
        )
        return (grad_query, grad_key, grad_value)

    grad_query_heads, grad_key_heads, grad_value_heads = lax.map(
        backward_head, (queries, key_heads, values, log_totals, grad_mixed)
    )
    _, rotate_pull = jax.vjp(lambda tensor: rotate(tensor, cosine, sine), attn_pre[:, 0])
    grad_query_pre = rotate_pull(jnp.transpose(grad_query_heads, (1, 0, 2)))[0]
    grad_key_pre = rotate_pull(jnp.transpose(grad_key_heads, (1, 0, 2)))[0]
    grad_attn = jnp.stack(
        [grad_query_pre, grad_key_pre, jnp.transpose(grad_value_heads, (1, 0, 2))], axis=1
    )
    grad_attn = grad_attn.reshape(seq_len, attn_width).astype(jnp.bfloat16)
    grad_joint = jnp.concatenate([grad_attn, grad_hidden], axis=1)
    shard_rows = lax.all_gather(grad_joint, "col", axis=0, tiled=True)
    row_count = shard_rows.shape[0]
    product = jnp.einsum("tf,cf->tc", shard_rows, w_joint, preferred_element_type=jnp.float32)
    partial_in = product
    row_block = normed_all
    grad_weight = jnp.einsum("tc,tf->cf", row_block, shard_rows, preferred_element_type=jnp.float32)
    grad_bias = jnp.dot(
        jnp.ones((row_count,), jnp.bfloat16), shard_rows, preferred_element_type=jnp.float32
    )
    partial_in, grad_w_in, grad_b_in = (partial_in, grad_weight, grad_bias)
    grad_normed = lax.psum_scatter(partial_in, "row", scatter_dimension=0, tiled=True)
    grad_scaled = grad_normed * gain_f
    ln_sums = lax.psum(
        (jnp.sum(grad_scaled, axis=1), jnp.sum(grad_scaled * centred, axis=1)), "col"
    )
    cotangent_f = cotangent.astype(jnp.float32)
    grad_input = (
        inv_std * (grad_scaled - ln_sums[0][:, None] / D - centred * ln_sums[1][:, None] / D)
        + cotangent_f
    )
    vectors = lax.psum(
        (
            jnp.sum(cotangent_f, axis=0),
            jnp.sum(grad_normed * centred, axis=0),
            jnp.sum(grad_normed, axis=0),
        ),
        ("dp", "row"),
    )
    weights = lax.psum((grad_w_in, grad_b_in, grad_w_out), "dp")
    grad_w_qkv = weights[0][:, :attn_width].reshape(w_qkv.shape)
    grad_b_qkv = weights[1][:attn_width].reshape(b_qkv.shape)
    grad_w_fc1 = weights[0][:, attn_width:]
    grad_b_fc1 = weights[1][attn_width:]
    grad_w_dense = weights[2][:mixed_width]
    grad_w_fc2 = weights[2][mixed_width:]
    return (
        output,
        grad_input,
        grad_w_qkv,
        grad_b_qkv,
        grad_w_fc1,
        grad_b_fc1,
        grad_w_dense,
        grad_w_fc2,
        vectors[0],
        vectors[1],
        vectors[2],
    )


def solution(mesh):
    in_specs = (
        P(("dp", "row"), "col"),
        P(("dp", "row"), "col"),
        P(("dp", "col"), None),
        P("col", None, "row"),
        P(None, "row"),
        P("col", "row"),
        P("row"),
        P("row", "col"),
        P("row", "col"),
        P("col"),
        P("col"),
        P("col"),
    )
    out_specs = (
        P(("dp", "row"), "col"),
        P(("dp", "row"), "col"),
        P("col", None, "row"),
        P(None, "row"),
        P("col", "row"),
        P("row"),
        P("row", "col"),
        P("row", "col"),
        P("col"),
        P("col"),
        P("col"),
    )
    return jax.shard_map(shards, mesh=mesh, in_specs=in_specs, out_specs=out_specs, check_vma=False)
```

profile of v0, /device:TPU:0, one launch (start us, length us, event | category | flops | bytes accessed | tf_op | source)
XLA Modules:
  0.0 1172.4 jit_solution(5631145118066468936)
XLA Ops:
  9.7 13.5 %all-reduce.8 = (f32[256]{0:T(256)S(1)}, f32[256]{0:T(256)S(1)}) all-reduce(f32[256]{0:T(256)S(1)} %get-tuple-element.209, f32[256]{0:T(256)S(1)} %get-tuple-element.208), channel_id=1, replica_groups=mesh['dp'=2,'row'=4,'col'=4] {'col'}, use_global_device_ids=true, to_apply=%region_3.0 | all-reduce | flops 512 | bytes 4096 | tf_op jit(solution)/shard_map/psum | solution.py:53
  23.2 1.8 fusion.68
  25.9 1.7 copy.36
  27.6 12.5 %all-gather.5.cloned.1.call-done = bf16[1024,512]{1,0:T(8,128)(2,1)} async-done(((bf16[256,512]{1,0:T(8,128)(2,1)}), bf16[1024,512]{1,0:T(8,128)(2,1)}) %all-gather.5.cloned.1.call-update) | async-done | bytes 1048592 | tf_op jit(solution)/shard_map/all_gather | solution.py:60
  40.1 5.6 fusion.87
  47.0 7.3 fusion.88
  56.2 3.1 constant_dynamic-update-slice_fusion
  59.3 9.6 convolution_bitcast_fusion.2
  70.5 101.0 %reduce-scatter.6.cloned.1.call-done = f32[256,1536]{1,0:T(8,128)} async-done(((f32[1024,1536]{1,0:T(8,128)}), f32[256,1536]{1,0:T(8,128)}) %reduce-scatter.6.cloned.1.call-update) | async-done | bytes 1572880 | tf_op jit(solution)/shard_map/reduce_scatter | solution.py:68
  171.5 147.4 %reduce-scatter.8.cloned.1.call-done = f32[256,2048]{1,0:T(8,128)} async-done(((f32[1024,2048]{1,0:T(8,128)}), f32[256,2048]{1,0:T(8,128)}) %reduce-scatter.8.cloned.1.call-update) | async-done | bytes 2097168 | tf_op jit(solution)/shard_map/reduce_scatter | solution.py:75
  318.9 2.5 maximum_add_fusion
  321.4 1.8 copy-done
  323.4 1.6 copy.37
  330.2 4.7 while.30
  335.0 164.8 %reduce-scatter.12.cloned.1.call-done = f32[256,2560]{1,0:T(8,128)} async-done(((f32[1024,2560]{1,0:T(8,128)}), f32[256,2560]{1,0:T(8,128)}) %reduce-scatter.12.cloned.1.call-update) | async-done | bytes 2621456 | tf_op jit(solution)/shard_map/reduce_scatter | solution.py:126
  499.8 2.0 convert_element_type.88
  502.6 2.6 fusion.54
  505.9 1.8 copy.43
  507.7 44.8 %while.31 = (s32[]{:T(128)}, f32[8,256,64]{1,2,0:T(8,128)}, f32[8,256,64]{1,2,0:T(8,128)}, bf16[8,256,64]{1,2,0:T(8,128)(2,1)S(1)}, bf16[8,256,64]{2,1,0:T(8,128...) while((s32[]{:T(128)}, f32[8,256,64]{1,2,0:T(8,128)}, ...), condition=%wide.region_16.17_spmd.clone.clone, body=%wide.region_14.16_spmd.clone.sunk.clone | while | flops 42761984 | bytes 2568305 | solution.py:171
  511.6 1.7 fusion.153
  517.2 1.7 fusion.153
  522.8 1.7 fusion.153
  528.4 1.7 fusion.153
  534.0 1.7 fusion.153
  539.6 1.7 fusion.153
  545.2 1.7 fusion.153
  550.8 1.7 fusion.153
  556.6 1.4 copy.48
  558.0 1.4 pad_maximum_fusion
  562.7 130.5 %all-gather.11.cloned.1.call-done = bf16[1024,3584]{1,0:T(8,128)(2,1)} async-done(((bf16[256,3584]{1,0:T(8,128)(2,1)}), bf16[1024,3584]{1,0:T(8,128)(2,1)}) %all-gather.11.cloned.1.call-update) | async-done | bytes 7340048 | tf_op jit(solution)/shard_map/all_gather | solution.py:182
  693.1 9.0 fusion.48
  702.2 89.3 %all-gather.7.cloned.1.call-done = bf16[1024,2560]{1,0:T(8,128)(2,1)} async-done(((bf16[256,2560]{1,0:T(8,128)(2,1)}), bf16[1024,2560]{1,0:T(8,128)(2,1)}) %all-gather.7.cloned.1.call-update) | async-done | bytes 5242896 | tf_op jit(solution)/shard_map/all_gather | solution.py:119
  791.5 7.5 fusion.89
  799.3 7.9 fusion.91
  807.2 9.5 fusion.90
  817.4 4.2 convolution_reduce_fusion
  821.6 7.9 psum.75
  830.7 1.4 fusion.73
  832.1 8.7 all-reduce.7
  840.8 17.7 %reduce-scatter.10.cloned.1.call-done = f32[256,512]{1,0:T(8,128)} async-done(((f32[1024,512]{1,0:T(8,128)}), f32[256,512]{1,0:T(8,128)}) %reduce-scatter.10.cloned.1.call-update) | async-done | bytes 524304 | tf_op jit(solution)/shard_map/reduce_scatter | solution.py:123
  858.5 2.3 convert_reduce_fusion.1
  860.8 13.9 %all-reduce.6 = (f32[512]{0:T(512)}, f32[512]{0:T(512)}, f32[512]{0:T(512)}) all-reduce(f32[512]{0:T(512)S(1)} %get-tuple-element.271, f32[512]{0:T(512)S(1)} %get-tuple-element.204, f32[512]{0:T(512)S(1)} %get-tuple-element.207), channel_id=1, replica_groups=mesh['dp'=2,'row'=4,'col'=4] {'dp','row'}, use_global_device_ids=true, to_apply=%region_26.27 | all-reduce | flops 1536 | bytes 12288 | tf_op jit(solution)/shard_map/psum | solution.py:202
  874.8 274.4 %all-reduce.12.cloned.1.call-done = (f32[512,3584]{1,0:T(8,128)}, f32[2560,512]{1,0:T(8,128)}) async-done(((f32[512,3584]{1,0:T(8,128)}, f32[2560,512]{1,0:T(8,128)}), (f32[512,3584]{1,0:T(8,128)}, f32[2560,512]{1,0:T(8,128)})) %all-reduce.12.cloned.1.call-update) | async-done | bytes 12582928 | tf_op jit(solution)/shard_map/psum | solution.py:210
  1149.1 2.3 slice.126
  1151.4 4.8 slice.127
  1157.3 2.4 slice.124
  1159.7 2.4 copy.50
  1162.0 3.5 copy.51
  (195 shorter events, 61.1 us)
Async XLA Ops:
  7.2 33.0 %all-gather.5.cloned.1.call-start = ((), (), s32[]{:S(2)}) async-start(), calls=%async_computation.5 | async-start | bytes 1310720 | tf_op jit(solution)/shard_map/all_gather | solution.py:60
  25.1 34.2 %all-gather.9.cloned.1.call-start = ((), (), s32[]{:S(2)}) async-start(), calls=%async_computation.10 | async-start | bytes 1310720 | tf_op jit(solution)/shard_map/all_gather | solution.py:61
  25.8 145.7 %reduce-scatter.6.cloned.1.call-start = ((), (), s32[]{:S(2)}) async-start(), calls=%async_computation.6 | async-start | bytes 7864320 | tf_op jit(solution)/shard_map/reduce_scatter | solution.py:68
  45.8 1.2 copy-start.11
  45.8 273.1 %reduce-scatter.8.cloned.1.call-start = ((), (), s32[]{:S(2)}) async-start(), calls=%async_computation.7 | async-start | bytes 10485760 | tf_op jit(solution)/shard_map/reduce_scatter | solution.py:75
  54.3 1.0 copy-start.14
  54.4 445.4 %reduce-scatter.12.cloned.1.call-start = ((), (), s32[]{:S(2)}) async-start(), calls=%async_computation.11 | async-start | bytes 13107200 | tf_op jit(solution)/shard_map/reduce_scatter | solution.py:126
  68.8 0.7 copy-start.15
  68.8 1.3 copy-start.16
  68.8 1.5 copy-start.17
  68.9 624.2 %all-gather.11.cloned.1.call-start = ((), (), s32[]{:S(2)}) async-start(), calls=%async_computation.12 | async-start | bytes 9175040 | tf_op jit(solution)/shard_map/all_gather | solution.py:182
  70.2 256.1 %copy-start.5 = (bf16[8,256,64]{1,2,0:T(8,128)(2,1)}, bf16[8,256,64]{1,2,0:T(8,128)(2,1)S(1)}, u32[]{:S(2)}) copy-start(bf16[8,256,64]{1,2,0:T(8,128)(2,1)S(1)} %fusion.86) | copy-start | bytes 786436
  321.4 1.8 copy-start
  326.3 3.9 copy-start.8
  335.0 164.9 %copy-start.7 = (bf16[8,256,64]{1,2,0:T(8,128)(2,1)}, bf16[8,256,64]{1,2,0:T(8,128)(2,1)S(1)}, u32[]{:S(2)}) copy-start(bf16[8,256,64]{1,2,0:T(8,128)(2,1)S(1)} %get-tuple-element.103) | copy-start | bytes 786436
  335.0 164.8 %copy-start.9 = (bf16[8,256,64]{2,1,0:T(8,128)(2,1)}, bf16[8,256,64]{2,1,0:T(8,128)(2,1)S(1)}, u32[]{:S(2)}) copy-start(bf16[8,256,64]{2,1,0:T(8,128)(2,1)S(1)} %get-tuple-element.529) | copy-start | bytes 786436
  335.0 164.8 %copy-start.10 = (bf16[8,256,64]{2,1,0:T(8,128)(2,1)}, bf16[8,256,64]{2,1,0:T(8,128)(2,1)S(1)}, u32[]{:S(2)}) copy-start(bf16[8,256,64]{2,1,0:T(8,128)(2,1)S(1)} %get-tuple-element.530) | copy-start | bytes 786436
  499.8 2.8 copy-start.1
  502.6 5.1 copy-start.6
  559.4 1.3 copy-start.3
  559.4 232.1 %all-gather.7.cloned.1.call-start = ((), (), s32[]{:S(2)}) async-start(), calls=%async_computation.8 | async-start | bytes 6553600 | tf_op jit(solution)/shard_map/all_gather | solution.py:119
  561.9 268.8 %reduce-scatter.14.cloned.1.call-start = ((), (), s32[]{:S(2)}) async-start(), calls=%async_computation.13 | async-start | bytes 2621440 | tf_op jit(solution)/shard_map/reduce_scatter | solution.py:192
  702.1 97.2 %copy-start.19 = (bf16[1024,512]{1,0:T(8,128)(2,1)S(1)}, bf16[1024,512]{1,0:T(8,128)(2,1)}, u32[]{:S(2)}) copy-start(bf16[1024,512]{1,0:T(8,128)(2,1)} %all-gather.9.cloned.1.call-done) | copy-start | bytes 3145732
  702.1 156.4 %reduce-scatter.10.cloned.1.call-start = ((), (), s32[]{:S(2)}) async-start(), calls=%async_computation.9 | async-start | bytes 2621440 | tf_op jit(solution)/shard_map/reduce_scatter | solution.py:123
  799.0 8.2 copy-start.12
  799.0 350.1 %all-reduce.12.cloned.1.call-start = ((), (), s32[]{:S(2)}) async-start(), calls=%async_computation.14 | async-start | bytes 25165824 | tf_op jit(solution)/shard_map/psum | solution.py:210
  816.7 0.7 copy-start.18
  817.4 13.4 %copy-start.4 = (bf16[256,512]{1,0:T(8,128)(2,1)S(1)}, bf16[256,512]{1,0:T(8,128)(2,1)}, u32[]{:S(2)}) copy-start(bf16[256,512]{1,0:T(8,128)(2,1)} %param.16) | copy-start | bytes 786436
  817.4 41.1 %copy-start.13 = (bf16[256,512]{1,0:T(8,128)(2,1)S(1)}, bf16[256,512]{1,0:T(8,128)(2,1)}, u32[]{:S(2)}) copy-start(bf16[256,512]{1,0:T(8,128)(2,1)} %param.17) | copy-start | bytes 786436
  1151.4 5.6 copy-start.2
Sparse Core Ops, SparseCore 0:
  25.2 14.8 all-gather.4
  41.7 16.6 all-gather.8
  60.7 110.7 reduce-scatter.5
  173.8 145.1 reduce-scatter.7
  321.1 178.6 reduce-scatter.11
  559.6 133.5 all-gather.10
  695.2 96.2 all-gather.6
  794.6 29.5 reduce-scatter.13
  827.3 31.1 reduce-scatter.9
  860.9 288.2 all-reduce.11
where the time goes:
time: 1180 us; the launch traced here: 1170 us
  waiting for transfers between devices  939 us (80%)
  matrix products  108 us (9%)
  blocking collectives  44 us (4%)
  local copies, waits for them, and re-layouts  43.5 us (4%)
  other arithmetic  22.4 us (2%)
  between operations  14.5 us (1%)
    psum x1, waiting for transfers between devices, shards(): weights = lax.psum((grad_w_in, grad_b_in, grad_w_out), 'dp')  274 us
    reduce_scatter x1, waiting for transfers between devices, shards(): lax.psum_scatter(jnp.einsum('tc,fc->tf', row_block, w_out, preferred_elem...  165 us
    reduce_scatter x1, waiting for transfers between devices, shards(): lax.psum_scatter(jnp.dot(row_block, w_fc1, preferred_element_type=jnp.flo...  147 us
    all_gather x1, waiting for transfers between devices, shards(): shard_rows = lax.all_gather(grad_joint, 'col', axis=0, tiled=True)  130 us
    reduce_scatter x1, waiting for transfers between devices, shards(): lax.psum_scatter(jnp.dot(row_block, w_attn, preferred_element_type=jnp.fl...  101 us
    all_gather x1, waiting for transfers between devices, shards(): lax.all_gather(branch_in, 'col', axis=0, tiled=True)  89.3 us
  transfers between devices with their start and end apart: 10, of which 8 were waited for; matrix products, arithmetic and copies ran while one was open for 8% of the time, Pallas kernels for 0%

commit v1 on v0

v1 whole, which is shorter than its diff:
```python
import functools
import math

import jax
import jax.numpy as jnp
from jax import lax
from jax.experimental import pallas as pl
from jax.experimental.pallas import tpu as pltpu
from jax.sharding import PartitionSpec as P

HEAD_DIM = 64
ROT = 32
epsilon = 1e-05
masked_score = -1e30
f32 = jnp.float32
bf16 = jnp.bfloat16
C0 = math.sqrt(2.0 / math.pi)
C1 = 0.044715


def dot(a, b, ca, cb):
    return lax.dot_general(a, b, (((ca,), (cb,)), ((), ())), preferred_element_type=f32)


def rotary_tables(segments):
    length = segments.shape[1]
    position = jnp.arange(length, dtype=jnp.int32)
    boundary = jnp.concatenate(
        [jnp.ones((segments.shape[0], 1), dtype=bool), segments[:, 1:] != segments[:, :-1]], axis=1
    )
    segment_start = lax.cummax(jnp.where(boundary, position[None], 0), axis=1)
    offset = (position[None] - segment_start).astype(f32)
    half_width = ROT // 2
    inverse = 10000.0 ** (-(2.0 * jnp.arange(half_width, dtype=f32)) / ROT)
    angles = offset[..., None] * inverse
    cosine, sine = jnp.cos(angles), jnp.sin(angles)
    zero = jnp.zeros_like(sine)
    rest = jnp.zeros(angles.shape[:2] + (HEAD_DIM - ROT,), f32)
    own = jnp.concatenate([cosine, cosine, rest + 1.0], axis=-1)
    above = jnp.concatenate([-sine, zero, rest], axis=-1)
    below = jnp.concatenate([zero, sine, rest], axis=-1)
    return [jnp.concatenate([t, t], axis=-1) for t in (own, above, below)]


def remote(src, dst, send, recv, where):
    return pltpu.make_async_remote_copy(
        src_ref=src, dst_ref=dst, send_sem=send, recv_sem=recv, device_id=where, device_id_type=pl.DeviceIdType.MESH
    )


def greet(others):
    barrier = pltpu.get_barrier_semaphore()
    count = 0
    for cond, where in others:
        if cond is True:
            pl.semaphore_signal(barrier, inc=1, device_id=where, device_id_type=pl.DeviceIdType.MESH)
            count += 1
        else:

            @pl.when(cond)
            def _():
                pl.semaphore_signal(barrier, inc=1, device_id=where, device_id_type=pl.DeviceIdType.MESH)

            count += cond.astype(jnp.int32)
    pl.semaphore_wait(barrier, count)


def gather_kernel(both_ref, all_ref, lsem, zs, zr, xs, xr, ys, yr, cs, cr):
    _, n, dz = both_ref.shape
    nc = all_ref.shape[2] // dz
    nr = lax.axis_size("row")
    x, r, z = lax.axis_index("dp"), lax.axis_index("row"), lax.axis_index("col")
    xp, yp, cp = {"dp": 1 - x}, {"row": lax.rem(r + 2, nr)}, {"row": r + 1 - 2 * lax.rem(r, 2)}
    left, right = {"col": z - 1}, {"col": z + 1}
    greet([(True, xp), (True, yp), (True, cp), (z > 0, left), (z < nc - 1, right)])

    def item(g, zz):
        return all_ref.at[:, pl.ds(pl.multiple_of(g * n, n), n), pl.ds(pl.multiple_of(zz * dz, dz), dz)]

    rp, rc = lax.rem(r + 2, nr), r + 1 - 2 * lax.rem(r, 2)
    rcp = lax.rem(rc + 2, nr)
    mine = [x * nr + r, (1 - x) * nr + r, x * nr + rp, (1 - x) * nr + rp]
    theirs = [x * nr + rc, (1 - x) * nr + rc, x * nr + rcp, (1 - x) * nr + rcp]

    def each(body):
        for s in range(nc):
            for zz in [z] if s == 0 else [z - s, z + s]:
                if s == 0:
                    body(s, zz)
                else:

                    @pl.when((zz >= 0) & (zz < nc))
                    def _():
                        body(s, zz)

    keep = pltpu.make_async_copy(both_ref, item(mine[0], z), lsem)
    keep.start()

    def to_left(src, zz):
        return remote(src, item(mine[0], zz), zs.at[0, zz], zr.at[zz], left)

    def to_right(src, zz):
        return remote(src, item(mine[0], zz), zs.at[1, zz], zr.at[zz], right)

    def to_x(k, src, g, zz):
        return remote(src, item(g, zz), xs.at[k, zz], xr.at[k, zz], xp)

    def to_y(k, src, g, zz):
        return remote(src, item(g, zz), ys.at[k, zz], yr.at[k, zz], yp)

    def to_core(k, src, g, zz):
        return remote(src, item(g, zz), cs.at[k, zz], cr.at[k, zz], cp)

    def first(s, zz):
        src = both_ref if s == 0 else item(mine[0], zz)
        if s > 0:
            to_left(src, zz).wait_recv()

        @pl.when((zz >= z) & (z > 0))
        def _():
            to_left(src, zz).start()

        @pl.when((zz <= z) & (z < nc - 1))
        def _():
            to_right(src, zz).start()

        to_x(0, src, mine[0], zz).start()
        to_y(0, src, mine[0], zz).start()
        to_core(0, src, mine[0], zz).start()

    each(first)

    def second(s, zz):
        even = lax.rem(zz, 2) == 0
        a, b = item(mine[1], zz), item(mine[2], zz)
        to_x(0, a, mine[1], zz).wait_recv()

        @pl.when(even)
        def _():
            to_y(1, a, mine[1], zz).start()

        to_core(1, a, mine[1], zz).start()
        to_y(0, b, mine[2], zz).wait_recv()

        @pl.when(jnp.logical_not(even))
        def _():
            to_x(1, b, mine[2], zz).start()

        to_core(2, b, mine[2], zz).start()

    each(second)

    def third(s, zz):
        even = lax.rem(zz, 2) == 0
        d = item(mine[3], zz)

        @pl.when(even)
        def _():
            to_y(1, d, mine[3], zz).wait_recv()

        @pl.when(jnp.logical_not(even))
        def _():
            to_x(1, d, mine[3], zz).wait_recv()

        to_core(3, d, mine[3], zz).start()

    each(third)
    keep.wait()

    def last(s, zz):
        even = lax.rem(zz, 2) == 0
        src = both_ref
        for k in range(4):
            to_core(k, src, theirs[k], zz).wait_recv()
            to_core(k, src, theirs[k], zz).wait_send()
        to_x(0, src, mine[0], zz).wait_send()
        to_y(0, src, mine[0], zz).wait_send()

        @pl.when(even)
        def _():
            to_y(1, src, mine[1], zz).wait_send()

        @pl.when(jnp.logical_not(even))
        def _():
            to_x(1, src, mine[2], zz).wait_send()

        @pl.when((zz >= z) & (z > 0))
        def _():
            to_left(src, zz).wait_send()

        @pl.when((zz <= z) & (z < nc - 1))
        def _():
            to_right(src, zz).wait_send()

    each(last)


def tail_kernel(
    D, part_ref, gpart_ref, both_ref, stat_ref, gain_ref, bias_ref,
    out_ref, gin_ref, vec_ref,
    cbuf, b1, b2, zbuf, vbuf, cs, cr, s1s, s1r, s2s, s2r, zs, zr, vs, vr,
):
    _, n, dz = both_ref.shape
    nd, nr, nc = lax.axis_size("dp"), lax.axis_size("row"), lax.axis_size("col")
    x, r, z = lax.axis_index("dp"), lax.axis_index("row"), lax.axis_index("col")
    y, c = r // 2, lax.rem(r, 2)
    xp, yp, cp = {"dp": 1 - x}, {"row": lax.rem(r + 2, nr)}, {"row": r + 1 - 2 * c}
    along_z = [{"col": lax.rem(z + k, nc)} for k in range(1, nc)]
    me = x * nr + r
    npl = nd * nr
    plane = []
    for k in range(1, npl):
        g = lax.rem(me + k, npl)
        plane.append({"dp": g // nr, "row": lax.rem(g, nr)})
    greet([(True, w) for w in along_z + plane])

    def rows(xx, yy, cc):
        return pl.ds(pl.multiple_of((xx * nr + yy * 2 + cc) * n, n), n)

    arrays = [part_ref, gpart_ref]
    places = [(x, y), (1 - x, y), (x, 1 - y), (1 - x, 1 - y)]

    core = [[remote(arrays[a].at[rows(*places[k], 1 - c)], cbuf.at[a, k], cs.at[a, k], cr.at[a, k], cp) for k in range(4)] for a in range(2)]
    order = [(0, 1), (0, 3), (1, 2), (1, 3), (0, 2), (1, 1), (0, 0), (1, 0)]
    for a, k in order:
        core[a][k].start()

    def chip_sum(a, k):
        core[a][k].wait_recv()
        cbuf[a, k] = cbuf[a, k] + arrays[a][rows(*places[k], c), :]

    across = [xp, yp]
    far = [1, 2]
    one = [[None, None], [None, None]]
    for a in range(2):
        for j, k in enumerate([far[a], 3]):
            one[a][j] = remote(cbuf.at[a, k], b1.at[a, j], s1s.at[a, j], s1r.at[a, j], across[a])
    for a, k in order[:4]:
        chip_sum(a, k)
        one[a][0 if k == far[a] else 1].start()
    for a, k in order[4:]:
        chip_sum(a, k)
    two = []
    for a in range(2):
        k = far[1 - a]
        one[a][1].wait_recv()
        b1[a, 1] = b1[a, 1] + cbuf[a, k]
        two.append(remote(b1.at[a, 1], b2.at[a], s2s.at[a], s2r.at[a], across[1 - a]))
        two[a].start()
    for a in range(2):
        one[a][0].wait_recv()
        cbuf[a, 0] = cbuf[a, 0] + b1[a, 0]
    hid = both_ref[0].astype(f32)
    mean, inv = stat_ref[:, 0:1], stat_ref[:, 1:2]
    xhat = (hid - mean) * inv
    two[1].wait_recv()
    gn = cbuf[1, 0] + b2[1]
    gnx = gn * xhat
    g = gn * gain_ref[...]
    lane = lax.broadcasted_iota(jnp.int32, (n, 128), 1)
    sums = jnp.where(lane == 0, jnp.sum(g, axis=1, keepdims=True), jnp.sum(g * xhat, axis=1, keepdims=True))
    zbuf[z] = sums.T[:8]
    line = lax.broadcasted_iota(jnp.int32, (8, dz), 0)
    vbuf[me] = jnp.where(
        line == 0, jnp.sum(gnx, axis=0, keepdims=True), jnp.where(line == 1, jnp.sum(gn, axis=0, keepdims=True), 0.0)
    )
    zc = [remote(zbuf.at[z], zbuf.at[z], zs.at[k], zr.at[k], w) for k, w in enumerate(along_z)]
    for copy in zc:
        copy.start()
    vc = [remote(vbuf.at[me], vbuf.at[me], vs.at[k], vr.at[k], w) for k, w in enumerate(plane)]
    for copy in vc:
        copy.start()
    two[0].wait_recv()
    out_ref[...] = (hid + (cbuf[0, 0] + b2[0]) + bias_ref[...]).astype(bf16)
    for copy in zc:
        copy.wait()
    total = zbuf[0]
    for k in range(1, nc):
        total += zbuf[k]
    both = jnp.concatenate([total] * (128 // 8), axis=0).T
    gin_ref[...] = both_ref[1].astype(f32) + inv * (g - both[:, 0:1] / D - xhat * (both[:, 1:2] / D))
    for copy in vc:
        copy.wait()
    total = vbuf[0]
    for k in range(1, npl):
        total += vbuf[k]
    vec_ref[...] = total
    for a, k in order:
        core[a][k].wait_send()
    for a in range(2):
        one[a][0].wait_send()
        one[a][1].wait_send()
        two[a].wait_send()


def norm_kernel(both_ref, gain_ref, shift_ref, normed_ref, stat_ref):
    hid = both_ref[0].astype(f32)
    D = hid.shape[1]
    mean = jnp.sum(hid, axis=1, keepdims=True) / D
    cen = hid - mean
    inv = lax.rsqrt(jnp.sum(cen * cen, axis=1, keepdims=True) / D + epsilon)
    normed_ref[...] = (cen * inv * gain_ref[...] + shift_ref[...]).astype(bf16)
    lane = lax.broadcasted_iota(jnp.int32, stat_ref.shape, 1)
    stat_ref[...] = jnp.where(lane == 0, mean, inv)


def attn_kernel(
    normed_ref, cot_ref, wq_ref, wd_ref, bq_ref, own_ref, above_ref, below_ref, srow_ref, scol_ref,
    part_ref, gpart_ref, dwq_ref, dwd_ref, dbq_ref,
):
    s = pl.program_id(0)
    z = lax.axis_index("col")
    nz, aw, dz = wd_ref.shape
    seq = normed_ref.shape[0]
    heads = aw // HEAD_DIM
    local = pl.ds(pl.multiple_of(z * dz, dz), dz)
    wide = lambda r: jnp.concatenate([r[0]] * (aw // 128), axis=1)
    own, above, below = wide(own_ref), wide(above_ref), wide(below_ref)

    def rot(t):
        return t * own + pltpu.roll(t, aw - ROT // 2, 1) * above + pltpu.roll(t, ROT // 2, 1) * below

    def unrot(t):
        return t * own - pltpu.roll(t, aw - ROT // 2, 1) * above - pltpu.roll(t, ROT // 2, 1) * below

    proj = dot(normed_ref[...], wq_ref[...], 1, 0) + bq_ref[...]
    q = rot(proj[:, :aw]).astype(bf16)
    k = rot(proj[:, aw : 2 * aw]).astype(bf16)
    v = proj[:, 2 * aw :].astype(bf16)
    gm = jnp.zeros((seq, aw), f32)
    for i in range(nz):
        gm += dot(cot_ref[:, i * dz : (i + 1) * dz], wd_ref[i], 1, 1)
    gm = gm.astype(bf16)
    rows = lax.broadcasted_iota(jnp.int32, (seq, seq), 0)
    cols = lax.broadcasted_iota(jnp.int32, (seq, seq), 1)
    allowed = (scol_ref[0] == srow_ref[0]) & (rows >= cols)
    head_of = lax.broadcasted_iota(jnp.int32, (seq, aw), 1) // HEAD_DIM
    scale = HEAD_DIM ** (-0.5)
    mixed = jnp.zeros((seq, aw), f32)
    gq = jnp.zeros((seq, aw), f32)
    gk = jnp.zeros((seq, aw), f32)
    gv = jnp.zeros((seq, aw), f32)
    zero = jnp.zeros((seq, aw), bf16)
    for h in range(heads):
        mine = head_of == h
        qh = jnp.where(mine, q, zero)
        kh = jnp.where(mine, k, zero)
        vh = jnp.where(mine, v, zero)
        gh = jnp.where(mine, gm, zero)
        scores = jnp.where(allowed, dot(qh, k, 1, 1) * scale, masked_score)
        peak = jnp.max(scores, axis=1, keepdims=True)
        ex = jnp.exp(scores - peak)
        soft = ex * (1.0 / jnp.sum(ex, axis=1, keepdims=True))
        probs = soft.astype(bf16)
        mixed += dot(probs, vh, 1, 0)
        gp = dot(gh, v, 1, 1)
        centre = jnp.sum(soft * gp, axis=1, keepdims=True)
        gs = (soft * (gp - centre)).astype(bf16)
        gq += dot(gs, kh, 1, 0)
        gk += dot(gs, qh, 0, 0)
        gv += dot(probs, gh, 0, 0)
    mixed = mixed.astype(bf16)
    g = jnp.concatenate([unrot(gq * scale), unrot(gk * scale), gv], axis=1).astype(bf16)
    cot_loc = cot_ref[:, local]
    normed_loc = normed_ref[:, local]
    part_ref[...] = dot(mixed, wd_ref[z], 1, 0)
    gpart_ref[...] = dot(g, wq_ref[local, :], 1, 1)

    @pl.when(s == 0)
    def _():
        dwq_ref[...] = jnp.zeros_like(dwq_ref)
        dwd_ref[...] = jnp.zeros_like(dwd_ref)
        dbq_ref[...] = jnp.zeros_like(dbq_ref)

    dwq_ref[...] += dot(normed_loc, g, 0, 0)
    dwd_ref[...] += dot(mixed, cot_loc, 0, 0)
    dbq_ref[...] += jnp.sum(g.astype(f32), axis=0, keepdims=True)


def mlp_kernel(
    normed_ref, cot_ref, w1_ref, w2_ref, b1_ref, part_in, gpart_in,
    part_ref, gpart_ref, dw1_ref, dw2_ref, db1_ref, act_s, gh_s,
):
    s = pl.program_id(0)
    z = lax.axis_index("col")
    nz, fw, dz = w2_ref.shape
    tb = normed_ref.shape[0]
    local = pl.ds(pl.multiple_of(z * dz, dz), dz)
    fb = 256
    for j in range(fw // fb):
        fs = slice(j * fb, (j + 1) * fb)
        u = dot(normed_ref[...], w1_ref[:, fs], 1, 0) + b1_ref[:, fs]
        ga = jnp.zeros((tb, fb), f32)
        for i in range(nz):
            ga += dot(cot_ref[:, i * dz : (i + 1) * dz], w2_ref[i, fs, :], 1, 1)
        ga = ga.astype(bf16).astype(f32)
        u2 = u * u
        t = jnp.tanh(C0 * (u + C1 * (u2 * u)))
        cdf = 0.5 * (1.0 + t)
        act_s[:, fs] = (u * cdf).astype(bf16)
        slope = cdf + (0.5 * u) * (1.0 - t * t) * (C0 * (1.0 + (3.0 * C1) * u2))
        gh_s[:, fs] = (slope * ga).astype(bf16)
    act, gh = act_s[...], gh_s[...]
    cot_loc = cot_ref[:, local]
    normed_loc = normed_ref[:, local]
    part_ref[...] = part_in[...] + dot(act, w2_ref[z], 1, 0)
    gpart_ref[...] = gpart_in[...] + dot(gh, w1_ref[local, :], 1, 1)

    @pl.when(s == 0)
    def _():
        dw1_ref[...] = jnp.zeros_like(dw1_ref)
        dw2_ref[...] = jnp.zeros_like(dw2_ref)
        db1_ref[...] = jnp.zeros_like(db1_ref)

    dw1_ref[...] += dot(normed_loc, gh, 0, 0)
    dw2_ref[...] += dot(act, cot_loc, 0, 0)
    db1_ref[...] += jnp.sum(gh.astype(f32), axis=0, keepdims=True)


def shape(s, d):
    return jax.ShapeDtypeStruct(s, d)


def whole(s):
    return pl.BlockSpec(s, lambda i: (0,) * len(s))


def shards(hidden_in, cotangent, segment_ids, w_qkv, b_qkv, w_fc1, b_fc1, w_dense, w_fc2, out_bias, ln_gain, ln_shift):
    nd, nr, nc = lax.axis_size("dp"), lax.axis_size("row"), lax.axis_size("col")
    x, z = lax.axis_index("dp"), lax.axis_index("col")
    seq_len = segment_ids.shape[1]
    nloc, dz = hidden_in.shape
    D = dz * nc
    T = nloc * nd * nr
    nseq = T // seq_len
    aw = w_qkv.shape[2] // nd
    fw = w_fc1.shape[1] // nd
    half = lambda w, n, axis: lax.dynamic_slice_in_dim(w, x * n, n, axis)

    both = jnp.stack([hidden_in, cotangent])
    dma = pltpu.SemaphoreType.DMA
    pair = pl.pallas_call(
        gather_kernel,
        in_specs=[pl.BlockSpec(memory_space=pl.ANY)],
        out_specs=pl.BlockSpec(memory_space=pl.ANY),
        out_shape=shape((2, T, D), bf16),
        scratch_shapes=[
            dma, dma((2, nc)), dma((nc,)), dma((2, nc)), dma((2, nc)), dma((2, nc)), dma((2, nc)), dma((4, nc)), dma((4, nc)),
        ],
        compiler_params=pltpu.CompilerParams(collective_id=0, has_side_effects=True),
        name="gather",
    )(both)
    segs = lax.all_gather(segment_ids, ("dp", "col"), axis=0, tiled=True)
    gain_all, shift_all = lax.all_gather(jnp.stack([ln_gain, ln_shift]), "col", axis=1, tiled=True).astype(f32)

    wq = half(w_qkv, aw, 2).reshape(dz, 3 * aw)
    wd = half(w_dense, aw, 0)
    w1 = half(w_fc1, fw, 1)
    w2 = half(w_fc2, fw, 0)
    bq = half(b_qkv, aw, 1).astype(f32).reshape(1, 3 * aw)
    b1 = half(b_fc1, fw, 0).astype(f32).reshape(1, fw)
    wq_all = lax.all_gather(wq, "col", axis=0, tiled=True)
    wd_all = lax.all_gather(wd, "col", axis=0)
    nchunk = 2
    fc = fw // nchunk
    w1_all = [lax.all_gather(w1[:, i * fc : (i + 1) * fc], "col", axis=0, tiled=True) for i in range(nchunk)]
    w2_all = [lax.all_gather(w2[i * fc : (i + 1) * fc], "col", axis=0) for i in range(nchunk)]

    nb = min(256, seq_len)
    normed, stat = pl.pallas_call(
        norm_kernel,
        grid=(T // nb,),
        in_specs=[pl.BlockSpec((1, nb, D), lambda i: (0, i, 0)), whole((1, D)), whole((1, D))],
        out_specs=[pl.BlockSpec((nb, D), lambda i: (i, 0)), pl.BlockSpec((nb, 128), lambda i: (i, 0))],
        out_shape=[shape((T, D), bf16), shape((T, 128), f32)],
        name="norm",
    )(pair, gain_all.reshape(1, D), shift_all.reshape(1, D))

    tables = rotary_tables(segs)
    cot_blk = lambda n: pl.BlockSpec((None, n, D), lambda i: (1, i, 0))
    blk = lambda n, w: pl.BlockSpec((n, w), lambda i: (i, 0))
    seq_blk = lambda a, b: pl.BlockSpec((1, a, b), lambda i: (i, 0, 0))
    part, gpart, dwq, dwd, dbq = pl.pallas_call(
        attn_kernel,
        grid=(nseq,),
        in_specs=[
            blk(seq_len, D), cot_blk(seq_len), whole((D, 3 * aw)), whole((nc, aw, dz)), whole((1, 3 * aw)),
            seq_blk(seq_len, 128), seq_blk(seq_len, 128), seq_blk(seq_len, 128), seq_blk(1, seq_len), seq_blk(seq_len, 1),
        ],
        out_specs=[blk(seq_len, dz), blk(seq_len, dz), whole((dz, 3 * aw)), whole((aw, dz)), whole((1, 3 * aw))],
        out_shape=[
            shape((T, dz), f32), shape((T, dz), f32), shape((dz, 3 * aw), f32), shape((aw, dz), f32), shape((1, 3 * aw), f32),
        ],
        name="attn",
    )(normed, pair, wq_all, wd_all, bq, *tables, segs[:, None, :], segs[:, :, None])

    tb = 512
    dw1s, dw2s, db1s = [], [], []
    for i in range(nchunk):
        part, gpart, a, b, c = pl.pallas_call(
            mlp_kernel,
            grid=(T // tb,),
            in_specs=[
                blk(tb, D), cot_blk(tb), whole((D, fc)), whole((nc, fc, dz)), whole((1, fc)), blk(tb, dz), blk(tb, dz),
            ],
            out_specs=[blk(tb, dz), blk(tb, dz), whole((dz, fc)), whole((fc, dz)), whole((1, fc))],
            out_shape=[shape((T, dz), f32), shape((T, dz), f32), shape((dz, fc), f32), shape((fc, dz), f32), shape((1, fc), f32)],
            scratch_shapes=[pltpu.VMEM((tb, fc), bf16), pltpu.VMEM((tb, fc), bf16)],
            name="mlp",
        )(normed, pair, w1_all[i], w2_all[i], b1[:, i * fc : (i + 1) * fc], part, gpart)
        dw1s.append(a)
        dw2s.append(b)
        db1s.append(c)

    me = lax.axis_index(("dp", "row"))
    stat_l = lax.dynamic_slice_in_dim(stat, me * nloc, nloc, 0)
    vmem = pl.BlockSpec(memory_space=pltpu.VMEM)
    npl = nd * nr
    output, grad_input, vec = pl.pallas_call(
        functools.partial(tail_kernel, D),
        in_specs=[vmem] * 6,
        out_specs=[vmem] * 3,
        out_shape=[shape((nloc, dz), bf16), shape((nloc, dz), f32), shape((8, dz), f32)],
        scratch_shapes=[
            pltpu.VMEM((2, 4, nloc, dz), f32), pltpu.VMEM((2, 2, nloc, dz), f32), pltpu.VMEM((2, nloc, dz), f32),
            pltpu.VMEM((nc, 8, nloc), f32), pltpu.VMEM((npl, 8, dz), f32),
            dma((2, 4)), dma((2, 4)), dma((2, 2)), dma((2, 2)), dma((2,)), dma((2,)),
            dma((nc - 1,)), dma((nc - 1,)), dma((npl - 1,)), dma((npl - 1,)),
        ],
        compiler_params=pltpu.CompilerParams(collective_id=1, has_side_effects=True),
        name="tail",
    )(part, gpart, both, stat_l, ln_gain.astype(f32).reshape(1, dz), out_bias.astype(f32).reshape(1, dz))
    cot_loc = lax.dynamic_slice(pair, (1, 0, z * dz), (1, T, dz))[0]
    d_ob = jnp.sum(cot_loc.astype(f32), axis=0)

    ag = lambda a, axis: lax.all_gather(a, "dp", axis=axis, tiled=True)
    return (
        output,
        grad_input,
        ag(dwq.reshape(dz, 3, aw), 2),
        ag(dbq.reshape(3, aw), 1),
        ag(jnp.concatenate(dw1s, axis=1), 1),
        ag(jnp.concatenate(db1s, axis=1)[0], 0),
        ag(dwd, 0),
        ag(jnp.concatenate(dw2s, axis=0), 0),
        d_ob,
        vec[0],
        vec[1],
    )


def solution(mesh):
    in_specs = (
        P(("dp", "row"), "col"), P(("dp", "row"), "col"), P(("dp", "col"), None), P("col", None, "row"), P(None, "row"),
        P("col", "row"), P("row"), P("row", "col"), P("row", "col"), P("col"), P("col"), P("col"),
    )
    out_specs = (
        P(("dp", "row"), "col"), P(("dp", "row"), "col"), P("col", None, "row"), P(None, "row"), P("col", "row"), P("row"),
        P("row", "col"), P("row", "col"), P("col"), P("col"), P("col"),
    )
    return jax.shard_map(shards, mesh=mesh, in_specs=in_specs, out_specs=out_specs, check_vma=False)
```

time: 1180 us -> 534 us (0.45)
  waiting for transfers between devices: 939 us -> 120 us
  Pallas kernels: 0 us -> 289 us
  matrix products: 108 us -> 0 us
    reduce_scatter x5 -> x0, waiting for transfers between devices: 431 us -> none  [the longest x1 165 us: shards(): lax.psum_scatter(jnp.einsum('tc,fc->tf', row_block, w_out, preferred_elem...]
    pallas_call x0 -> x6, Pallas kernels: none -> 289 us  [the longest x1 124 us: shards(): pl.pallas_call(gather_kernel, in_specs=[pl.BlockSpec(memory_space=pl.ANY)...]
    psum x1 -> x0, waiting for transfers between devices: 274 us -> none  [shards(): weights = lax.psum((grad_w_in, grad_b_in, grad_w_out), 'dp')]
    all_gather x4 -> x10, waiting for transfers between devices: 232 us -> 119 us  [the longest x4 88.4 us: shards(): ag = lambda a, axis: lax.all_gather(a, 'dp', axis=axis, tiled=True)]
    dot_general x64 -> x0, matrix products: 108 us -> none  [the longest x8 13.4 us: backward_head(): jnp.dot(grad_scores, key_head, preferred_element_type=jnp.float32)]
    all_gather x0 -> x4, blocking collectives: none -> 44.7 us  [the longest x1 23 us: shards(): segs = lax.all_gather(segment_ids, ('dp', 'col'), axis=0, tiled=True)]
    psum x4 -> x0, blocking collectives: 44 us -> none  [the longest x1 13.9 us: shards(): lax.psum((jnp.sum(cotangent_f, axis=0), jnp.sum(grad_normed * centred, ax...]
  transfers between devices with their start and end apart: 10 -> 10, of which waited for: 8 -> 3; matrix products, arithmetic and copies ran while one was open for 8% -> 9% of each run, Pallas kernels for 0% -> 54%
where the time goes in v1:
time: 534 us; the launch traced here: 533 us
  Pallas kernels  289 us (54%)
  waiting for transfers between devices  120 us (22%)
  local copies, waits for them, and re-layouts  48.1 us (9%)
  blocking collectives  44.7 us (8%)
  other arithmetic  15.5 us (3%)
  between operations  14.5 us (3%)
    pallas_call x1, Pallas kernels, shards(): pl.pallas_call(gather_kernel, in_specs=[pl.BlockSpec(memory_space=pl.ANY)...  124 us
    all_gather x4, waiting for transfers between devices, shards(): ag = lambda a, axis: lax.all_gather(a, 'dp', axis=axis, tiled=True)  88.4 us
    pallas_call x1, Pallas kernels, shards(): pl.pallas_call(functools.partial(tail_kernel, D), in_specs=[vmem] * 6, ou...  72.1 us
    pallas_call x2, Pallas kernels, shards(): pl.pallas_call(mlp_kernel, grid=(T // tb,), in_specs=[blk(tb, D), cot_blk...  44 us
    pallas_call x1, Pallas kernels, shards(): pl.pallas_call(attn_kernel, grid=(nseq,), in_specs=[blk(seq_len, D), cot_...  37.4 us
    all_gather x2, waiting for transfers between devices, shards(): lax.all_gather(w2[i * fc:(i + 1) * fc], 'col', axis=0)  30.8 us
    all_gather x1, blocking collectives, shards(): segs = lax.all_gather(segment_ids, ('dp', 'col'), axis=0, tiled=True)  23 us
    unnamed x53, local copies, waits for them, and re-layouts  17.7 us
  transfers between devices with their start and end apart: 10, of which 3 were waited for; matrix products, arithmetic and copies ran while one was open for 9% of the time, Pallas kernels for 54%

profile of v1, /device:TPU:0, one launch (start us, length us, event | category | flops | bytes accessed | tf_op | source)
XLA Modules:
  0.0 532.7 jit_solution(16074056834135876444)
XLA Ops:
  7.2 1.8 constant_dynamic-slice_fusion.4
  9.5 1.2 copy.32
  10.7 2.2 constant_dynamic-slice_fusion.7
  13.0 2.3 constant_dynamic-slice_fusion.6
  15.4 0.5 all-gather.16.cloned.1.call-update
  16.6 23.0 %all-gather.4.srow_ref = s32[8,1,256]{2,1,0:T(1,128)S(1)} all-gather(s32[1,1,256]{2,1,0:T(1,128)S(1)} %bitcast.40), channel_id=1, replica_groups=mesh['dp'=2,'row'=4,'col'=4] {'dp','col'}, dimensions={0}, use_global_device_ids=true | all-gather | bytes 9216 | tf_op jit(solution)/shard_map/all_gather | solution.py:453
  39.6 0.6 copy.38
  40.2 0.8 pad_maximum_fusion.2.both_ref
  41.1 124.1 %gather.1.both_ref.cot_ref = bf16[2,2048,2048]{2,1,0:T(8,128)(2,1)} custom-call(bf16[2,256,512]{2,1,0:T(8,128)(2,1)} %pad_maximum_fusion.2.both_ref), custom_call_target="tpu_custom_call" | custom-call | tf_op jit(solution)/shard_map/gather/pallas_call | solution.py:442
  165.4 0.6 reduce-window.6
  166.3 5.5 %multiply_sine_fusion = (f32[8,256,16]{2,1,0:T(8,128)}, f32[8,256,16]{2,1,0:T(8,128)}, f32[8,256,16]{2,1,0:T(8,128)S(1)}) fusion(f32[16]{0:T(128)S(1)} %multiply_power_fusion, f32[8,256]{1,0:T(8,128)S(1)} %fusion.1), kind=kLoop, calls=%fused_computation.3 | loop fusion | flops 65536 | bytes 401472 | tf_op jit(solution)/shard_map/sin | solution.py:36
  171.9 1.1 broadcast_in_dim.28
  172.9 5.1 concatenate.29.above_ref
  178.0 4.7 concatenate.30.below_ref
  182.7 1.4 broadcast_in_dim.31.scol_ref
  184.2 3.0 concatenate.28.own_ref
  187.2 12.6 %all_gather.51 = bf16[2,2048]{1,0:T(2,128)(2,1)S(1)} all-gather(bf16[2,512]{1,0:T(2,128)(2,1)S(1)} %pad_maximum_fusion.4), channel_id=1, replica_groups=mesh['dp'=2,'row'=4,'col'=4] {'col'}, dimensions={1}, use_global_device_ids=true | all-gather | bytes 10240 | tf_op jit(solution)/shard_map/all_gather | solution.py:454
  199.7 0.6 fusion.3
  200.4 11.3 %norm.1 = (bf16[2048,2048]{1,0:T(8,128)(2,1)}, f32[2048,128]{1,0:T(8,128)}) custom-call(bf16[2,2048,2048]{2,1,0:T(8,128)(2,1)} %gather.1.both_ref.cot_ref, f32[1,2048]{1,0:T(1,128)} %get-tuple-element.83.gain_ref, f32[1,2048]{1,0:T(1,128)} %get-tuple-element.82.shift_ref), custom_call_target="tpu_custom_call" | custom-call | tf_op jit(solution)/shard_map/norm/pallas_call | solution.py:470
  211.7 37.4 %attn.1 = (f32[2048,512]{1,0:T(8,128)}, f32[2048,512]{1,0:T(8,128)}, f32[512,768]{1,0:T(8,128)}, f32[256,512]{1,0:T(8,128)}, f32[1,768]{1,0:T(1,128)}) custom-call(bf16[2048,2048]{1,0:T(8,128)(2,1)} %get-tuple-element.31.normed_ref, bf16[2,2048,2048]{2,1,0:T(8,128)(2,1)} %gather.1.both_ref.cot_ref, bf16[2048,768]{1,0:T(8,128)(2,1)} %all-gather.20.cloned.1.call-done.wq_ref, ...), custom_call_target="tpu_custom_call" | custom-call | tf_op jit(solution)/shard_map/attn/pallas_call | solution.py:483
  249.2 3.1 copy.34
  252.5 0.6 fusion.4
  253.1 22.0 %mlp.2 = (f32[2048,512]{1,0:T(8,128)}, f32[2048,512]{1,0:T(8,128)}, f32[512,512]{1,0:T(8,128)}, f32[512,512]{1,0:T(8,128)}, f32[1,512]{1,0:T(1,128)}) custom-call(bf16[2048,2048]{1,0:T(8,128)(2,1)} %get-tuple-element.31.normed_ref, bf16[2,2048,2048]{2,1,0:T(8,128)(2,1)} %gather.1.both_ref.cot_ref, bf16[2048,512]{1,0:T(8,128)(2,1)} %all-gather.18.cloned.1.call-done.w1_ref, ...), custom_call_target="tpu_custom_call" | custom-call | tf_op jit(solution)/shard_map/mlp/pallas_call | solution.py:500
  275.1 30.8 %all-gather.30.cloned.1.call-done = bf16[2048,512]{1,0:T(8,128)(2,1)} async-done(((bf16[512,512]{1,0:T(8,128)(2,1)}), bf16[2048,512]{1,0:T(8,128)(2,1)}) %all-gather.30.cloned.1.call-update) | async-done | bytes 2097168 | tf_op jit(solution)/shard_map/all_gather | solution.py:467
  306.0 22.0 %mlp.3 = (f32[2048,512]{1,0:T(8,128)}, f32[2048,512]{1,0:T(8,128)}, f32[512,512]{1,0:T(8,128)}, f32[512,512]{1,0:T(8,128)}, f32[1,512]{1,0:T(1,128)}) custom-call(bf16[2048,2048]{1,0:T(8,128)(2,1)} %get-tuple-element.31.normed_ref, bf16[2,2048,2048]{2,1,0:T(8,128)(2,1)} %gather.1.both_ref.cot_ref, bf16[2048,512]{1,0:T(8,128)(2,1)} %all-gather.16.cloned.1.call-done.w1_ref, ...), custom_call_target="tpu_custom_call" | custom-call | tf_op jit(solution)/shard_map/mlp/pallas_call | solution.py:500
  328.0 2.7 pad_maximum_fusion.1
  330.8 1.1 copy-done.4
  332.3 1.6 pad_maximum_fusion
  333.9 0.6 copy-done.18
  334.5 0.6 reshape.100
  335.1 2.8 convert_reduce_fusion
  337.9 0.6 reshape_convert_fusion.gain_ref
  338.5 1.6 constant_dynamic-slice_fusion.2.stat_ref
  340.1 4.6 all-gather.3
  344.6 72.1 %tail.1 = (bf16[256,512]{1,0:T(8,128)(2,1)}, f32[256,512]{1,0:T(8,128)}, f32[8,512]{1,0:T(8,128)}) custom-call(f32[2048,512]{1,0:T(8,128)} %get-tuple-element.36.part_ref, f32[2048,512]{1,0:T(8,128)} %get-tuple-element.37.gpart_ref, bf16[2,256,512]{2,1,0:T(8,128)(2,1)} %pad_maximum_fusion.2.both_ref, f32[256,128]{1,0:T(8,128)} %constant_dynamic-slice_fusion.2.stat_ref, ...), custom_call_target="tpu_custom_call" | custom-call | tf_op jit(solution)/shard_map/tail/pallas_call | solution.py:519
  416.8 4.6 all_gather.63
  421.4 1.4 fusion.2
  422.8 3.6 copy.35
  426.4 29.6 %all-gather.28.cloned.1.call-done = f32[2048,512]{1,0:T(8,128)} async-done(((f32[1024,512]{1,0:T(8,128)}), f32[2048,512]{1,0:T(8,128)}) %all-gather.28.cloned.1.call-update) | async-done | bytes 4194320 | tf_op jit(solution)/shard_map/all_gather | solution.py:536
  456.0 58.8 %all-gather.24.cloned.1.call-done = f32[512,2048]{1,0:T(8,128)} async-done(((f32[512,1024]{1,0:T(8,128)}), f32[512,2048]{1,0:T(8,128)}) %all-gather.24.cloned.1.call-update) | async-done | bytes 4194320 | tf_op jit(solution)/shard_map/all_gather | solution.py:536
  514.8 0.7 copy.48
  515.5 0.8 copy.49
  516.3 0.6 copy.50
  516.9 4.8 copy.51
  521.8 0.6 copy.52
  522.4 1.0 copy.53
  523.3 2.0 copy.54
  525.4 0.5 copy-done.1
  (86 shorter events, 2.8 us)
Async XLA Ops:
  7.2 1.9 copy-start
  7.2 204.5 %all-gather.34.cloned.1.call-start = ((), (), s32[]{:S(2)}) async-start(), calls=%async_computation.9 | async-start | bytes 1310720 | tf_op jit(solution)/shard_map/all_gather | solution.py:463
  9.1 202.6 %all-gather.20.cloned.1.call-start = ((), (), s32[]{:S(2)}) async-start(), calls=%async_computation.2 | async-start | bytes 3932160 | tf_op jit(solution)/shard_map/all_gather | solution.py:462
  10.6 242.5 %all-gather.18.cloned.1.call-start = ((), (), s32[]{:S(2)}) async-start(), calls=%async_computation.1 | async-start | bytes 2621440 | tf_op jit(solution)/shard_map/all_gather | solution.py:466
  12.9 3.7 copy-start.16
  12.9 26.7 %copy-start.19 = (bf16[3,512]{1,0:T(4,128)(2,1)S(1)}, bf16[3,512]{1,0:T(4,128)(2,1)}, u32[]{:S(2)}) copy-start(bf16[3,512]{1,0:T(4,128)(2,1)} %param.16) | copy-start | bytes 9220
  12.9 27.3 %copy-start.9 = (bf16[256,512]{1,0:T(8,128)(2,1)S(1)}, bf16[256,512]{1,0:T(8,128)(2,1)}, u32[]{:S(2)}) copy-start(bf16[256,512]{1,0:T(8,128)(2,1)} %param.13) | copy-start | bytes 786436
  13.0 27.3 %copy-start.10 = (bf16[256,512]{1,0:T(8,128)(2,1)S(1)}, bf16[256,512]{1,0:T(8,128)(2,1)}, u32[]{:S(2)}) copy-start(bf16[256,512]{1,0:T(8,128)(2,1)} %param.12) | copy-start | bytes 786436
  13.0 240.2 %all-gather.32.cloned.1.call-start = ((), (), s32[]{:S(2)}) async-start(), calls=%async_computation.8 | async-start | bytes 2621440 | tf_op jit(solution)/shard_map/all_gather | solution.py:467
  15.4 259.7 %all-gather.16.cloned.1.call-start = ((), (), s32[]{:S(2)}) async-start(), calls=%async_computation | async-start | bytes 2621440 | tf_op jit(solution)/shard_map/all_gather | solution.py:466
  16.0 290.0 %all-gather.30.cloned.1.call-start = ((), (), s32[]{:S(2)}) async-start(), calls=%async_computation.7 | async-start | bytes 2621440 | tf_op jit(solution)/shard_map/all_gather | solution.py:467
  16.6 406.2 %all-gather.26.cloned.1.call-start = ((), (), s32[]{:S(2)}) async-start(), calls=%async_computation.5 | async-start | bytes 1572864 | tf_op jit(solution)/shard_map/all_gather | solution.py:536
  39.6 125.6 %copy-start.11 = (s32[8,1,256]{2,1,0:T(1,128)}, s32[8,1,256]{2,1,0:T(1,128)S(1)}, u32[]{:S(2)}) copy-start(s32[8,1,256]{2,1,0:T(1,128)S(1)} %all-gather.4.srow_ref) | copy-start | bytes 24580
  41.1 124.1 %copy-start.12 = (bf16[512]{0:T(512)(128)(2,1)S(1)}, bf16[512]{0:T(512)(128)(2,1)}, u32[]{:S(2)}) copy-start(bf16[512]{0:T(512)(128)(2,1)} %param.22) | copy-start | bytes 3076
  41.1 124.1 %copy-start.17 = (bf16[512]{0:T(512)(128)(2,1)S(1)}, bf16[512]{0:T(512)(128)(2,1)}, u32[]{:S(2)}) copy-start(bf16[512]{0:T(512)(128)(2,1)} %param.23) | copy-start | bytes 3076
  249.1 173.7 %all-gather.22.cloned.1.call-start = ((), (), s32[]{:S(2)}) async-start(), calls=%async_computation.3 | async-start | bytes 4718592 | tf_op jit(solution)/shard_map/all_gather | solution.py:536
  249.2 3.4 copy-start.20
  252.3 203.8 %all-gather.28.cloned.1.call-start = ((), (), s32[]{:S(2)}) async-start(), calls=%async_computation.6 | async-start | bytes 6291456 | tf_op jit(solution)/shard_map/all_gather | solution.py:536
  306.0 22.1 %copy-start.5 = (f32[512,512]{1,0:T(8,128)S(1)}, f32[512,512]{1,0:T(8,128)}, u32[]{:S(2)}) copy-start(f32[512,512]{1,0:T(8,128)} %get-tuple-element.48) | copy-start | bytes 3145732
  330.8 1.2 copy-start.4
  330.8 1.5 copy-start.6
  330.8 184.0 %all-gather.24.cloned.1.call-start = ((), (), s32[]{:S(2)}) async-start(), calls=%async_computation.4 | async-start | bytes 6291456 | tf_op jit(solution)/shard_map/all_gather | solution.py:536
  333.9 0.7 copy-start.18
  333.9 6.2 %copy-start.14 = (f32[1,512]{1,0:T(1,128)S(1)}, f32[1,512]{1,0:T(1,128)}, u32[]{:S(2)}) copy-start(f32[1,512]{1,0:T(1,128)} %get-tuple-element.45) | copy-start | bytes 6148
  333.9 6.2 %copy-start.15 = (f32[1,512]{1,0:T(1,128)S(1)}, f32[1,512]{1,0:T(1,128)}, u32[]{:S(2)}) copy-start(f32[1,512]{1,0:T(1,128)} %get-tuple-element.46) | copy-start | bytes 6148
  344.6 72.1 %copy-start.13 = (f32[1,768]{1,0:T(1,128)S(1)}, f32[1,768]{1,0:T(1,128)}, u32[]{:S(2)}) copy-start(f32[1,768]{1,0:T(1,128)} %get-tuple-element.42) | copy-start | bytes 9220
  422.8 92.0 %copy-start.8 = (bf16[256,512]{1,0:T(8,128)(2,1)S(1)}, bf16[256,512]{1,0:T(8,128)(2,1)}, u32[]{:S(2)}) copy-start(bf16[256,512]{1,0:T(8,128)(2,1)} %get-tuple-element.97) | copy-start | bytes 786436
  422.8 92.8 %copy-start.7 = (f32[256,512]{1,0:T(8,128)S(1)}, f32[256,512]{1,0:T(8,128)}, u32[]{:S(2)}) copy-start(f32[256,512]{1,0:T(8,128)} %get-tuple-element.98) | copy-start | bytes 1572868
  516.9 5.5 %copy-start.3 = (f32[512,512]{1,0:T(8,128)S(1)}, f32[512,512]{1,0:T(8,128)}, u32[]{:S(2)}) copy-start(f32[512,512]{1,0:T(8,128)} %all-gather.26.cloned.1.call-done) | copy-start | bytes 3145732
  516.9 6.4 %copy-start.2 = (f32[2048,512]{1,0:T(8,128)S(1)}, f32[2048,512]{1,0:T(8,128)}, u32[]{:S(2)}) copy-start(f32[2048,512]{1,0:T(8,128)} %all-gather.28.cloned.1.call-done) | copy-start | bytes 12582916
  523.3 2.5 copy-start.1
Sparse Core Ops, SparseCore 0:
  10.1 30.8 all-gather.33
  43.1 78.5 all-gather.19
  123.3 44.7 all-gather.17
  169.5 44.5 all-gather.31
  215.5 44.4 all-gather.15
  261.5 44.4 all-gather.29
  307.5 20.0 all-gather.25
  329.2 65.1 all-gather.21
  395.9 60.1 all-gather.27
  457.4 57.3 all-gather.23

commit v2 on v1

--- a/solution.py
+++ b/solution.py
@@ -22,26 +22,6 @@
     return lax.dot_general(a, b, (((ca,), (cb,)), ((), ())), preferred_element_type=f32)
 
 
-def rotary_tables(segments):
-    length = segments.shape[1]
-    position = jnp.arange(length, dtype=jnp.int32)
-    boundary = jnp.concatenate(
-        [jnp.ones((segments.shape[0], 1), dtype=bool), segments[:, 1:] != segments[:, :-1]], axis=1
-    )
-    segment_start = lax.cummax(jnp.where(boundary, position[None], 0), axis=1)
-    offset = (position[None] - segment_start).astype(f32)
-    half_width = ROT // 2
-    inverse = 10000.0 ** (-(2.0 * jnp.arange(half_width, dtype=f32)) / ROT)
-    angles = offset[..., None] * inverse
-    cosine, sine = jnp.cos(angles), jnp.sin(angles)
-    zero = jnp.zeros_like(sine)
-    rest = jnp.zeros(angles.shape[:2] + (HEAD_DIM - ROT,), f32)
-    own = jnp.concatenate([cosine, cosine, rest + 1.0], axis=-1)
-    above = jnp.concatenate([-sine, zero, rest], axis=-1)
-    below = jnp.concatenate([zero, sine, rest], axis=-1)
-    return [jnp.concatenate([t, t], axis=-1) for t in (own, above, below)]
-
-
 def remote(src, dst, send, recv, where):
     return pltpu.make_async_remote_copy(
         src_ref=src, dst_ref=dst, send_sem=send, recv_sem=recv, device_id=where, device_id_type=pl.DeviceIdType.MESH
@@ -65,25 +45,34 @@
     pl.semaphore_wait(barrier, count)
 
 
-def gather_kernel(both_ref, all_ref, lsem, zs, zr, xs, xr, ys, yr, cs, cr):
+def gather_kernel(
+    both_ref, wq_ref, wd_ref, small_ref, all_ref, wq_all, wd_all, small_all,
+    lsem, zs, zr, xs, xr, ys, yr, cs, cr, as_, ar, ss, sr,
+):
     _, n, dz = both_ref.shape
-    nc = all_ref.shape[2] // dz
-    nr = lax.axis_size("row")
+    nd, nr, nc = lax.axis_size("dp"), lax.axis_size("row"), wd_all.shape[0]
+    aw = wd_all.shape[1]
     x, r, z = lax.axis_index("dp"), lax.axis_index("row"), lax.axis_index("col")
-    xp, yp, cp = {"dp": 1 - x}, {"row": lax.rem(r + 2, nr)}, {"row": r + 1 - 2 * lax.rem(r, 2)}
+    rp, rc = lax.rem(r + 2, nr), r + 1 - 2 * lax.rem(r, 2)
+    rcp = lax.rem(rc + 2, nr)
+    xp, yp, cp = {"dp": 1 - x}, {"row": rp}, {"row": rc}
     left, right = {"col": z - 1}, {"col": z + 1}
-    greet([(True, xp), (True, yp), (True, cp), (z > 0, left), (z < nc - 1, right)])
+    ns = nd * nc
+    me = x * nc + z
+    others = []
+    for k in range(1, ns):
+        o = lax.rem(me + k, ns)
+        others.append({"dp": o // nc, "col": lax.rem(o, nc)})
+    greet([(True, yp), (True, cp)] + [(True, o) for o in others])
 
     def item(g, zz):
         return all_ref.at[:, pl.ds(pl.multiple_of(g * n, n), n), pl.ds(pl.multiple_of(zz * dz, dz), dz)]
 
-    rp, rc = lax.rem(r + 2, nr), r + 1 - 2 * lax.rem(r, 2)
-    rcp = lax.rem(rc + 2, nr)
     mine = [x * nr + r, (1 - x) * nr + r, x * nr + rp, (1 - x) * nr + rp]
     theirs = [x * nr + rc, (1 - x) * nr + rc, x * nr + rcp, (1 - x) * nr + rcp]
 
-    def each(body):
-        for s in range(nc):
+    def each(body, steps=range(nc)):
+        for s in steps:
             for zz in [z] if s == 0 else [z - s, z + s]:
                 if s == 0:
                     body(s, zz)
@@ -93,14 +82,27 @@
                     def _():
                         body(s, zz)
 
-    keep = pltpu.make_async_copy(both_ref, item(mine[0], z), lsem)
-    keep.start()
+    wd_own = wd_ref.at[pl.ds(pl.multiple_of(x * aw, aw), aw), :]
+    wq_at = lambda zz: wq_all.at[pl.ds(pl.multiple_of(zz * dz, dz), dz), :]
+    keeps = [
+        pltpu.make_async_copy(both_ref, item(mine[0], z), lsem.at[0]),
+        pltpu.make_async_copy(wq_ref, wq_at(z), lsem.at[1]),
+        pltpu.make_async_copy(wd_own, wd_all.at[z], lsem.at[2]),
+        pltpu.make_async_copy(small_ref, small_all.at[me], lsem.at[3]),
+    ]
+    tiny = [remote(small_ref, small_all.at[me], ss.at[k], sr.at[k], o) for k, o in enumerate(others)]
 
     def to_left(src, zz):
         return remote(src, item(mine[0], zz), zs.at[0, zz], zr.at[zz], left)
 
     def to_right(src, zz):
         return remote(src, item(mine[0], zz), zs.at[1, zz], zr.at[zz], right)
+
+    def weights(d, own, zz):
+        return [
+            remote(wq_ref if own else wq_at(zz), wq_at(zz), as_.at[0, d, zz], ar.at[0, zz], [left, right][d]),
+            remote(wd_own if own else wd_all.at[zz], wd_all.at[zz], as_.at[1, d, zz], ar.at[1, zz], [left, right][d]),
+        ]
 
     def to_x(k, src, g, zz):
         return remote(src, item(g, zz), xs.at[k, zz], xr.at[k, zz], xp)
@@ -128,7 +130,20 @@
         to_y(0, src, mine[0], zz).start()
         to_core(0, src, mine[0], zz).start()
 
-    each(first)
+    def pass_weights(s, zz):
+        if s > 0:
+            for copy in weights(0, False, zz):
+                copy.wait_recv()
+
+        @pl.when((zz >= z) & (z > 0))
+        def _():
+            for copy in weights(0, s == 0, zz):
+                copy.start()
+
+        @pl.when((zz <= z) & (z < nc - 1))
+        def _():
+            for copy in weights(1, s == 0, zz):
+                copy.start()
 
     def second(s, zz):
         even = lax.rem(zz, 2) == 0
@@ -148,8 +163,6 @@
 
         to_core(2, b, mine[2], zz).start()
 
-    each(second)
-
     def third(s, zz):
         even = lax.rem(zz, 2) == 0
         d = item(mine[3], zz)
@@ -164,8 +177,19 @@
 
         to_core(3, d, mine[3], zz).start()
 
+    each(first, range(1))
+    for copy in tiny + keeps:
+        copy.start()
+    each(first, range(1, nc))
+    each(pass_weights, range(1))
+    each(second)
+    each(pass_weights, range(1, 2))
     each(third)
-    keep.wait()
+    each(pass_weights, range(2, nc))
+    for copy in keeps:
+        copy.wait()
+    for copy in tiny:
+        copy.wait()
 
     def last(s, zz):
         even = lax.rem(zz, 2) == 0
@@ -186,11 +210,13 @@
 
         @pl.when((zz >= z) & (z > 0))
         def _():
-            to_left(src, zz).wait_send()
+            for copy in [to_left(src, zz)] + weights(0, True, zz):
+                copy.wait_send()
 
         @pl.when((zz <= z) & (z < nc - 1))
         def _():
-            to_right(src, zz).wait_send()
+            for copy in [to_right(src, zz)] + weights(1, True, zz):
+                copy.wait_send()
 
     each(last)
 
@@ -293,29 +319,46 @@
         two[a].wait_send()
 
 
-def norm_kernel(both_ref, gain_ref, shift_ref, normed_ref, stat_ref):
-    hid = both_ref[0].astype(f32)
-    D = hid.shape[1]
-    mean = jnp.sum(hid, axis=1, keepdims=True) / D
-    cen = hid - mean
-    inv = lax.rsqrt(jnp.sum(cen * cen, axis=1, keepdims=True) / D + epsilon)
-    normed_ref[...] = (cen * inv * gain_ref[...] + shift_ref[...]).astype(bf16)
-    lane = lax.broadcasted_iota(jnp.int32, stat_ref.shape, 1)
-    stat_ref[...] = jnp.where(lane == 0, mean, inv)
-
-
 def attn_kernel(
-    normed_ref, cot_ref, wq_ref, wd_ref, bq_ref, own_ref, above_ref, below_ref, srow_ref, scol_ref,
-    part_ref, gpart_ref, dwq_ref, dwd_ref, dbq_ref,
+    pair_ref, wq_ref, wd_ref, bq_ref, small_ref,
+    normed_ref, stat_ref, part_ref, gpart_ref, dwq_ref, dwd_ref, dbq_ref, dob_ref,
 ):
     s = pl.program_id(0)
     z = lax.axis_index("col")
     nz, aw, dz = wd_ref.shape
-    seq = normed_ref.shape[0]
+    seq, D = normed_ref.shape
     heads = aw // HEAD_DIM
     local = pl.ds(pl.multiple_of(z * dz, dz), dz)
-    wide = lambda r: jnp.concatenate([r[0]] * (aw // 128), axis=1)
-    own, above, below = wide(own_ref), wide(above_ref), wide(below_ref)
+    cot_ref = pair_ref.at[1]
+
+    hid = pair_ref[0].astype(f32)
+    mean = jnp.sum(hid, axis=1, keepdims=True) / D
+    cen = hid - mean
+    inv = lax.rsqrt(jnp.sum(cen * cen, axis=1, keepdims=True) / D + epsilon)
+    for i in range(nz):
+        cols = slice(i * dz, (i + 1) * dz)
+        xhat = cen[:, cols] * inv
+        normed_ref[:, cols] = (xhat * small_ref[i, 0:1, :dz] + small_ref[i, 1:2, :dz]).astype(bf16)
+    lane = lax.broadcasted_iota(jnp.int32, stat_ref.shape, 1)
+    stat_ref[...] = jnp.where(lane == 0, mean, inv)
+
+    rows = lax.broadcasted_iota(jnp.int32, (seq, seq), 0)
+    cols = lax.broadcasted_iota(jnp.int32, (seq, seq), 1)
+    srow = small_ref[s, 2:3, :seq]
+    scol = jnp.broadcast_to(srow, (8, seq)).T[:, 0:1]
+    same = scol == srow
+    allowed = same & (rows >= cols)
+    place = jnp.sum(jnp.where(same & (rows < cols), 1.0, 0.0), axis=0, keepdims=True)
+    hw = ROT // 2
+    freq = lax.broadcasted_iota(jnp.int32, (hw, seq), 0).astype(f32)
+    angle = place * jnp.exp(freq * (-2.0 * math.log(10000.0) / ROT))
+    cosine, sine = jnp.cos(angle), jnp.sin(angle)
+    zero = jnp.zeros((hw, seq), f32)
+    rest = jnp.zeros((HEAD_DIM - ROT, seq), f32)
+    wide = lambda ts: jnp.concatenate([jnp.concatenate(ts * 2, axis=0).T] * (aw // 128), axis=1)
+    own = wide([cosine, cosine, rest + 1.0])
+    above = wide([-sine, zero, rest])
+    below = wide([zero, sine, rest])
 
     def rot(t):
         return t * own + pltpu.roll(t, aw - ROT // 2, 1) * above + pltpu.roll(t, ROT // 2, 1) * below
@@ -331,9 +374,6 @@
     for i in range(nz):
         gm += dot(cot_ref[:, i * dz : (i + 1) * dz], wd_ref[i], 1, 1)
     gm = gm.astype(bf16)
-    rows = lax.broadcasted_iota(jnp.int32, (seq, seq), 0)
-    cols = lax.broadcasted_iota(jnp.int32, (seq, seq), 1)
-    allowed = (scol_ref[0] == srow_ref[0]) & (rows >= cols)
     head_of = lax.broadcasted_iota(jnp.int32, (seq, aw), 1) // HEAD_DIM
     scale = HEAD_DIM ** (-0.5)
     mixed = jnp.zeros((seq, aw), f32)
@@ -371,28 +411,511 @@
         dwq_ref[...] = jnp.zeros_like(dwq_ref)
         dwd_ref[...] = jnp.zeros_like(dwd_ref)
         dbq_ref[...] = jnp.zeros_like(dbq_ref)
-
+        dob_ref[...] = jnp.zeros_like(dob_ref)
+
+    dob_ref[...] += jnp.sum(cot_loc.astype(f32), axis=0, keepdims=True)
     dwq_ref[...] += dot(normed_loc, g, 0, 0)
     dwd_ref[...] += dot(mixed, cot_loc, 0, 0)
     dbq_ref[...] += jnp.sum(g.astype(f32), axis=0, keepdims=True)
 
 
-def mlp_kernel(
-    normed_ref, cot_ref, w1_ref, w2_ref, b1_ref, part_in, gpart_in,
-    part_ref, gpart_ref, dw1_ref, dw2_ref, db1_ref, act_s, gh_s,
+def attend(normed_ref, cot_ref, local, z, nz, wq, wd, bq_ref, srow, part_ref, gpart_ref, dwq_ref, dwd_ref, dbq_ref):
+    seq = normed_ref.shape[0]
+    aw, dz = dwd_ref.shape
+    heads = aw // HEAD_DIM
+    rows = lax.broadcasted_iota(jnp.int32, (seq, seq), 0)
+    cols = lax.broadcasted_iota(jnp.int32, (seq, seq), 1)
+    scol = jnp.broadcast_to(srow, (8, seq)).T[:, 0:1]
+    same = scol == srow
+    allowed = same & (rows >= cols)
+    place = jnp.sum(jnp.where(same & (rows < cols), 1.0, 0.0), axis=0, keepdims=True)
+    hw = ROT // 2
+    freq = lax.broadcasted_iota(jnp.int32, (hw, seq), 0).astype(f32)
+    angle = place * jnp.exp(freq * (-2.0 * math.log(10000.0) / ROT))
+    cosine, sine = jnp.cos(angle), jnp.sin(angle)
+    zero = jnp.zeros((hw, seq), f32)
+    rest = jnp.zeros((HEAD_DIM - ROT, seq), f32)
+    wide = lambda ts: jnp.concatenate([jnp.concatenate(ts * 2, axis=0).T] * (aw // 128), axis=1)
+    own = wide([cosine, cosine, rest + 1.0])
+    above = wide([-sine, zero, rest])
+    below = wide([zero, sine, rest])
+
+    def rot(t):
+        return t * own + pltpu.roll(t, aw - hw, 1) * above + pltpu.roll(t, hw, 1) * below
+
+    def unrot(t):
+        return t * own - pltpu.roll(t, aw - hw, 1) * above - pltpu.roll(t, hw, 1) * below
+
+    def across(ref, w, axis, width):
+        total = jnp.zeros((seq, width), f32)
+        for i in range(nz):
+            total += dot(ref[:, i * dz : (i + 1) * dz], w(i)[...], 1, axis)
+        return total
+
+    proj = across(normed_ref, wq, 0, 3 * aw) + bq_ref[...]
+    q = rot(proj[:, :aw]).astype(bf16)
+    k = rot(proj[:, aw : 2 * aw]).astype(bf16)
+    v = proj[:, 2 * aw :].astype(bf16)
+    gm = across(cot_ref, wd, 1, aw).astype(bf16)
+    head_of = lax.broadcasted_iota(jnp.int32, (seq, aw), 1) // HEAD_DIM
+    scale = HEAD_DIM ** (-0.5)
+    mixed = jnp.zeros((seq, aw), f32)
+    gq = jnp.zeros((seq, aw), f32)
+    gk = jnp.zeros((seq, aw), f32)
+    gv = jnp.zeros((seq, aw), f32)
+    none = jnp.zeros((seq, aw), bf16)
+    for h in range(heads):
+        mine = head_of == h
+        qh = jnp.where(mine, q, none)
+        kh = jnp.where(mine, k, none)
+        vh = jnp.where(mine, v, none)
+        gh = jnp.where(mine, gm, none)
+        scores = jnp.where(allowed, dot(qh, k, 1, 1) * scale, masked_score)
+        peak = jnp.max(scores, axis=1, keepdims=True)
+        ex = jnp.exp(scores - peak)
+        soft = ex * (1.0 / jnp.sum(ex, axis=1, keepdims=True))
+        probs = soft.astype(bf16)
+        mixed += dot(probs, vh, 1, 0)
+        gp = dot(gh, v, 1, 1)
+        centre = jnp.sum(soft * gp, axis=1, keepdims=True)
+        gs = (soft * (gp - centre)).astype(bf16)
+        gq += dot(gs, kh, 1, 0)
+        gk += dot(gs, qh, 0, 0)
+        gv += dot(probs, gh, 0, 0)
+    mixed = mixed.astype(bf16)
+    g = jnp.concatenate([unrot(gq * scale), unrot(gk * scale), gv], axis=1).astype(bf16)
+    part_ref[...] = dot(mixed, wd(z)[...], 1, 0)
+    gpart_ref[...] = dot(g, wq(z)[...], 1, 1)
+    dwq_ref[...] += dot(normed_ref[:, local], g, 0, 0)
+    dwd_ref[...] += dot(mixed, cot_ref[:, local], 0, 0)
+    dbq_ref[...] += jnp.sum(g.astype(f32), axis=0, keepdims=True)
+
+
+def hidden(normed_ref, cot_ref, local, z, nz, w1, w2, b1, part_ref, gpart_ref, dw1_ref, dw2_ref, db1_ref):
+    tb = normed_ref.shape[0]
+    dz, fc = dw1_ref.shape
+    u = jnp.zeros((tb, fc), f32)
+    ga = jnp.zeros((tb, fc), f32)
+    for i in range(nz):
+        cols = slice(i * dz, (i + 1) * dz)
+        u += dot(normed_ref[:, cols], w1(i)[...], 1, 0)
+        ga += dot(cot_ref[:, cols], w2(i)[...], 1, 1)
+    u += b1
+    ga = ga.astype(bf16).astype(f32)
+    u2 = u * u
+    t = jnp.tanh(C0 * (u + C1 * (u2 * u)))
+    cdf = 0.5 * (1.0 + t)
+    act = (u * cdf).astype(bf16)
+    slope = cdf + (0.5 * u) * (1.0 - t * t) * (C0 * (1.0 + (3.0 * C1) * u2))
+    gh = (slope * ga).astype(bf16)
+    part_ref[...] += dot(act, w2(z)[...], 1, 0)
+    gpart_ref[...] += dot(gh, w1(z)[...], 1, 1)
+    dw1_ref[...] += dot(normed_ref[:, local], gh, 0, 0)
+    dw2_ref[...] += dot(act, cot_ref[:, local], 0, 0)
+    db1_ref[...] += jnp.sum(gh.astype(f32), axis=0, keepdims=True)
+
+
+def layer_kernel(
+    both_ref, wq_ref, wd_ref, w1_ref, w2_ref, bq_ref, b1_ref, small_ref, gain_ref, bias_ref,
+    out_ref, gin_ref, vec_ref, gb_ref, gq_ref, gd_ref, g1_ref, g2_ref,
+    tok, wq_s, wd_s, w1_s, w2_s, part, gpart, dq, dd, d1, d2, stat, smalls, cbuf, ring1, ring2, zbuf, vbuf,
+    ksem, zs, zr, xs, xr, ys, yr, cs, cr, as_, ar, ms, mr, ts, tr, ds, dr, ls, bs, br,
+    rcs, rcr, r1s, r1r, r2s, r2r, zbs, zbr, vbs, vbr,
 ):
+    _, n, dz = both_ref.shape
+    nd, nr, nc = lax.axis_size("dp"), lax.axis_size("row"), lax.axis_size("col")
+    _, T, D = tok.shape
+    nj, _, _, fc = w1_s.shape
+    aw, fw = wd_s.shape[1], nj * fc
+    ns, npl = nd * nc, nd * nr
+    seq = n
+    x, r, z = lax.axis_index("dp"), lax.axis_index("row"), lax.axis_index("col")
+    y, c = r // 2, lax.rem(r, 2)
+    rp, rc = lax.rem(r + 2, nr), r + 1 - 2 * c
+    rcp = lax.rem(rc + 2, nr)
+    xp, yp, cp = {"dp": 1 - x}, {"row": rp}, {"row": rc}
+    beside = [{"col": z - 1}, {"col": z + 1}]
+    line, plane = [], []
+    for k in range(1, ns):
+        o = lax.rem(x * nc + z + k, ns)
+        line.append({"dp": o // nc, "col": lax.rem(o, nc)})
+    me = x * nr + r
+    for k in range(1, npl):
+        o = lax.rem(me + k, npl)
+        plane.append({"dp": o // nr, "row": lax.rem(o, nr)})
+    along = [{"col": lax.rem(z + k, nc)} for k in range(1, nc)]
+    greet([(True, w) for w in line + plane])
+
+    local = pl.ds(pl.multiple_of(z * dz, dz), dz)
+    at = lambda i, size: pl.ds(pl.multiple_of(i * size, size), size)
+
+    def item(g, zz):
+        return tok.at[:, at(g, n), at(zz, dz)]
+
+    mine = [x * nr + r, (1 - x) * nr + r, x * nr + rp, (1 - x) * nr + rp]
+    theirs = [x * nr + rc, (1 - x) * nr + rc, x * nr + rcp, (1 - x) * nr + rcp]
+
+    def each(body, steps=range(nc)):
+        for s in steps:
+            for zz in [z] if s == 0 else [z - s, z + s]:
+                if s == 0:
+                    body(s, zz)
+                else:
+
+                    @pl.when((zz >= 0) & (zz < nc))
+                    def _():
+                        body(s, zz)
+
+    def outward(zz, send):
+        @pl.when((zz >= z) & (z > 0))
+        def _():
+            send(0)
+
+        @pl.when((zz <= z) & (z < nc - 1))
+        def _():
+            send(1)
+
+    def tokens(d, s, zz):
+        src = both_ref if s == 0 else item(mine[0], zz)
+        return remote(src, item(mine[0], zz), zs.at[d, zz], zr.at[zz], beside[d])
+
+    wd_own = wd_ref.at[at(x, aw), :]
+    w1_own = lambda j: w1_ref.at[:, at(x * nj + j, fc)]
+    w2_own = lambda j: w2_ref.at[at(x * nj + j, fc), :]
+
+    def pieces(j, own, zz):
+        if j < 0:
+            a, b = wq_s.at[zz], wd_s.at[zz]
+            return [(wq_ref if own else a, a), (wd_own if own else b, b)]
+        a, b = w1_s.at[j, zz], w2_s.at[j, zz]
+        return [(w1_own(j) if own else a, a), (w2_own(j) if own else b, b)]
+
+    def weights(j, d, own, zz):
+        sems = [(as_.at[k, d, zz], ar.at[k, zz]) if j < 0 else (ms.at[k, d, j, zz], mr.at[k, j, zz]) for k in range(2)]
+        return [remote(a, b, *sems[k], beside[d]) for k, (a, b) in enumerate(pieces(j, own, zz))]
+
+    def pass_weights(j, steps, go=True):
+        def body(s, zz):
+            if s > 0:
+                for copy in weights(j, 0, False, zz):
+                    copy.wait_recv()
+
+            def send(d):
+                for copy in weights(j, d, s == 0, zz):
+                    copy.start()
+
+            if go:
+                outward(zz, send)
+
+        each(body, steps)
+
+    def to(sems, peer):
+        return lambda k, src, g, zz: remote(src, item(g, zz), sems[0].at[k, zz], sems[1].at[k, zz], peer)
+
+    to_x, to_y, to_core = to((xs, xr), xp), to((ys, yr), yp), to((cs, cr), cp)
+
+    def first(s, zz):
+        if s > 0:
+            tokens(0, s, zz).wait_recv()
+        outward(zz, lambda d: tokens(d, s, zz).start())
+        src = both_ref if s == 0 else item(mine[0], zz)
+        for send in (to_x, to_y, to_core):
+            send(0, src, mine[0], zz).start()
+
+    def second(s, zz):
+        even = lax.rem(zz, 2) == 0
+        a, b = item(mine[1], zz), item(mine[2], zz)
+        to_x(0, a, mine[1], zz).wait_recv()
+
+        @pl.when(even)
+        def _():
+            to_y(1, a, mine[1], zz).start()
+
+        to_core(1, a, mine[1], zz).start()
+        to_y(0, b, mine[2], zz).wait_recv()
+
+        @pl.when(jnp.logical_not(even))
+        def _():
+            to_x(1, b, mine[2], zz).start()
+
+        to_core(2, b, mine[2], zz).start()
+
+    def third(s, zz):
+        even = lax.rem(zz, 2) == 0
+        d = item(mine[3], zz)
+
+        @pl.when(even)
+        def _():
+            to_y(1, d, mine[3], zz).wait_recv()
+
+        @pl.when(jnp.logical_not(even))
+        def _():
+            to_x(1, d, mine[3], zz).wait_recv()
+
+        to_core(3, d, mine[3], zz).start()
+
+    def fourth(s, zz):
+        even = lax.rem(zz, 2) == 0
+        for k in range(4):
+            to_core(k, both_ref, theirs[k], zz).wait()
+        to_x(0, both_ref, mine[0], zz).wait_send()
+        to_y(0, both_ref, mine[0], zz).wait_send()
+
+        @pl.when(even)
+        def _():
+            to_y(1, both_ref, mine[1], zz).wait_send()
+
+        @pl.when(jnp.logical_not(even))
+        def _():
+            to_x(1, both_ref, mine[2], zz).wait_send()
+
+        outward(zz, lambda d: tokens(d, 0, zz).wait_send())
+
+    keeps = [(both_ref, item(mine[0], z)), (small_ref, smalls.at[x * nc + z]), *pieces(-1, True, z)]
+    for j in range(nj):
+        keeps += pieces(j, True, z)
+    keeps = [pltpu.make_async_copy(a, b, ksem.at[k]) for k, (a, b) in enumerate(keeps)]
+    tiny = [remote(small_ref, smalls.at[x * nc + z], ts.at[k], tr.at[k], w) for k, w in enumerate(line)]
+
+    each(first, range(1))
+    for copy in tiny + keeps:
+        copy.start()
+    each(first, range(1, nc))
+    pass_weights(-1, range(1))
+    each(second)
+    pass_weights(-1, range(1, 2))
+    pass_weights(0, range(1))
+    each(third)
+    for copy in keeps + tiny:
+        copy.wait()
+    each(fourth)
+
+    dq[...] = jnp.zeros_like(dq)
+    dd[...] = jnp.zeros_like(dd)
+    d1[...] = jnp.zeros_like(d1)
+    d2[...] = jnp.zeros_like(d2)
+    gb_ref[x] = jnp.zeros(gb_ref.shape[1:], f32)
+    vec_ref[...] = jnp.zeros_like(vec_ref)
+
+    def norm(s, _):
+        rows = at(s, seq)
+        hid = tok[0, rows, :].astype(f32)
+        mean = jnp.sum(hid, axis=1, keepdims=True) / D
+        cen = hid - mean
+        inv = lax.rsqrt(jnp.sum(cen * cen, axis=1, keepdims=True) / D + epsilon)
+        for i in range(nc):
+            cols = slice(i * dz, (i + 1) * dz)
+            xhat = cen[:, cols] * inv
+            tok[0, rows, cols] = (xhat * smalls[i, 0:1, :dz] + smalls[i, 1:2, :dz]).astype(bf16)
+        lane = lax.broadcasted_iota(jnp.int32, (seq, 128), 1)
+        stat[rows, :] = jnp.where(lane == 0, mean, inv)
+        vec_ref[2:3, :] += jnp.sum(tok[1, rows, local].astype(f32), axis=0, keepdims=True)
+        return 0
+
+    lax.fori_loop(0, T // seq, norm, 0)
+    pass_weights(-1, range(2, nc - 1))
+    pass_weights(-1, range(nc - 1, nc), go=False)
+    pass_weights(0, range(1, 2))
+    pass_weights(1, range(1))
+
+    def attn(s, _):
+        @pl.when(s == 3)
+        def _():
+            pass_weights(0, range(2, nc - 1))
+
+        @pl.when(s == 6)
+        def _():
+            pass_weights(1, range(1, 2))
+
+        rows = at(s, seq)
+        attend(
+            tok.at[0, rows, :], tok.at[1, rows, :], local, z, nc, lambda i: wq_s.at[i], lambda i: wd_s.at[i], bq_ref,
+            smalls[s, 2:3, :seq], part.at[rows, :], gpart.at[rows, :], dq, dd, gb_ref.at[x, 0, 0:1, : 3 * aw],
+        )
+        return 0
+
+    lax.fori_loop(0, T // seq, attn, 0)
+
+    def settle(k, src, dst):
+        return [remote(src, dst, ds.at[k], dr.at[k], xp), pltpu.make_async_copy(src, dst, ls.at[k])]
+
+    dqs = [settle(k, dq.at[:, k * aw : (k + 1) * aw], gq_ref.at[k, :, at(x, aw)]) for k in range(3)]
+    dense = settle(3, dd, gd_ref.at[at(x, aw), :])
+
+    def mlp_grads(j):
+        return settle(4 + 2 * j, d1.at[j], g1_ref.at[:, at(x * nj + j, fc)]) + settle(
+            5 + 2 * j, d2.at[j], g2_ref.at[at(x * nj + j, fc), :]
+        )
+
+    for copies in dqs + [dense]:
+        for copy in copies:
+            copy.start()
+
+    arrays = [part, gpart]
+    places = [(x, y), (1 - x, y), (x, 1 - y), (1 - x, 1 - y)]
+    rows_of = lambda k, cc: at(places[k][0] * nr + places[k][1] * 2 + cc, n)
+    core = [
+        [remote(arrays[a].at[rows_of(k, 1 - c), :], cbuf.at[a, k], rcs.at[a, k], rcr.at[a, k], cp) for k in range(4)]
+        for a in range(2)
+    ]
+    nb = 4
+    turn = [3, 1, 2, 0]
+    last = nj - 1
+    sends = {0: [(2, 0)], 4: [(1, 2), (3, 0)], 6: [(2, 1)], 8: [(2, 2)], 10: [(3, 1)], 12: [(3, 2)]}
+
+    def mlp(t, _):
+        j, b = t // nb, lax.rem(t, nb)
+        for k, todo in sends.items():
+
+            @pl.when(t == k)
+            def _():
+                for jj, s in todo:
+                    pass_weights(jj, range(s, s + 1))
+                if k % nb == 0:
+                    pass_weights(k // nb, range(nc - 1, nc), go=False)
+
+        xx = jnp.where((b == 0) | (b == 1), 1 - x, x)
+        yy = jnp.where((b == 0) | (b == 2), 1 - y, y)
+        rows = at(xx * (nr // 2) + yy, 2 * n)
+        hidden(
+            tok.at[0, rows, :], tok.at[1, rows, :], local, z, nc, lambda i: w1_s.at[j, i], lambda i: w2_s.at[j, i],
+            b1_ref[j], part.at[rows, :], gpart.at[rows, :], d1.at[j], d2.at[j], gb_ref.at[x, j + 1, 0:1, :fc],
+        )
+        for k in range(nb):
+
+            @pl.when(t == last * nb + k)
+            def _():
+                core[0][turn[k]].start()
+                core[1][turn[k]].start()
+
+        for jj in range(nj):
+
+            @pl.when(t == jj * nb + nb - 1)
+            def _():
+                if jj < last:
+                    for copy in mlp_grads(jj):
+                        copy.start()
+
+        return 0
+
+    lax.fori_loop(0, nj * nb, mlp, 0)
+
+    def chip_sum(a, k):
+        core[a][k].wait_recv()
+        cbuf[a, k] = cbuf[a, k] + arrays[a][rows_of(k, c), :]
+
+    over = [xp, yp]
+    far = [1, 2]
+    one = [
+        [remote(cbuf.at[a, k], ring1.at[a, i], r1s.at[a, i], r1r.at[a, i], over[a]) for i, k in enumerate([far[a], 3])]
+        for a in range(2)
+    ]
+    for i in (1, 0):
+        for a in range(2):
+            chip_sum(a, [far[a], 3][i])
+            one[a][i].start()
+    for copy in mlp_grads(last):
+        copy.start()
+    bias_copy = remote(gb_ref.at[x], gb_ref.at[x], bs, br, xp)
+    bias_copy.start()
+    for a in range(2):
+        chip_sum(a, far[1 - a])
+    for a in range(2):
+        chip_sum(a, 0)
+    two = []
+    for a in range(2):
+        one[a][1].wait_recv()
+        ring1[a, 1] = ring1[a, 1] + cbuf[a, far[1 - a]]
+        two.append(remote(ring1.at[a, 1], ring2.at[a], r2s.at[a], r2r.at[a], over[1 - a]))
+        two[a].start()
+    for a in range(2):
+        one[a][0].wait_recv()
+        cbuf[a, 0] = cbuf[a, 0] + ring1[a, 0]
+    hid = both_ref[0].astype(f32)
+    ours = stat[at(me, n), :]
+    mean, inv = ours[:, 0:1], ours[:, 1:2]
+    xhat = (hid - mean) * inv
+    two[1].wait_recv()
+    gn = cbuf[1, 0] + ring2[1]
+    g = gn * gain_ref[...]
+    lane = lax.broadcasted_iota(jnp.int32, (n, 128), 1)
+    sums = jnp.where(lane == 0, jnp.sum(g, axis=1, keepdims=True), jnp.sum(g * xhat, axis=1, keepdims=True))
+    zbuf[z] = sums.T[:8]
+    zc = [remote(zbuf.at[z], zbuf.at[z], zbs.at[k], zbr.at[k], w) for k, w in enumerate(along)]
+    for copy in zc:
+        copy.start()
+    which = lax.broadcasted_iota(jnp.int32, (8, dz), 0)
+    vbuf[me] = jnp.where(
+        which == 0,
+        jnp.sum(gn * xhat, axis=0, keepdims=True),
+        jnp.where(which == 1, jnp.sum(gn, axis=0, keepdims=True), 0.0),
+    )
+    vc = [remote(vbuf.at[me], vbuf.at[me], vbs.at[k], vbr.at[k], w) for k, w in enumerate(plane)]
+    for copy in vc:
+        copy.start()
+    two[0].wait_recv()
+    out_ref[...] = (hid + (cbuf[0, 0] + ring2[0]) + bias_ref[...]).astype(bf16)
+    for copy in zc:
+        copy.wait()
+    total = zbuf[0]
+    for k in range(1, nc):
+        total += zbuf[k]
+    total = jnp.concatenate([total] * (128 // 8), axis=0).T
+    gin_ref[...] = both_ref[1].astype(f32) + inv * (g - total[:, 0:1] / D - xhat * (total[:, 1:2] / D))
+    for copy in vc:
+        copy.wait()
+    total = vbuf[0]
+    for k in range(1, npl):
+        total += vbuf[k]
+    vec_ref[0:2, :] = total[0:2]
+
+    bias_copy.wait()
+    for a in range(2):
+        for k in range(4):
+            core[a][k].wait_send()
+        one[a][0].wait_send()
+        one[a][1].wait_send()
+        two[a].wait_send()
+    for copies in dqs + [dense] + [mlp_grads(j) for j in range(nj)]:
+        for copy in copies:
+            copy.wait()
+
+    def sent(s, zz):
+        def wait(d):
+            for j in range(-1, nj):
+                for copy in weights(j, d, True, zz):
+                    copy.wait_send()
+
+        outward(zz, wait)
+
+    each(sent)
+
+
+def mlp_kernel(joint, normed_ref, cot_ref, *refs):
+    if joint:
+        w_ref, *refs = refs
+        w1 = lambda i: w_ref.at[i, 0]
+        w2 = lambda i: w_ref.at[i, 1]
+    else:
+        w1_ref, w2_ref, *refs = refs
+        w1 = lambda i: w1_ref.at[i]
+        w2 = lambda i: w2_ref.at[i]
+    b1_ref, part_in, gpart_in, part_ref, gpart_ref, dw1_ref, dw2_ref, db1_ref, act_s, gh_s = refs
     s = pl.program_id(0)
     z = lax.axis_index("col")
-    nz, fw, dz = w2_ref.shape
+    dz, fw = dw1_ref.shape
+    nz = normed_ref.shape[1] // dz
     tb = normed_ref.shape[0]
     local = pl.ds(pl.multiple_of(z * dz, dz), dz)
     fb = 256
     for j in range(fw // fb):
         fs = slice(j * fb, (j + 1) * fb)
-        u = dot(normed_ref[...], w1_ref[:, fs], 1, 0) + b1_ref[:, fs]
+        u = b1_ref[:, fs] + jnp.zeros((tb, fb), f32)
+        for i in range(nz):
+            u += dot(normed_ref[:, i * dz : (i + 1) * dz], w1(i)[:, fs], 1, 0)
         ga = jnp.zeros((tb, fb), f32)
         for i in range(nz):
-            ga += dot(cot_ref[:, i * dz : (i + 1) * dz], w2_ref[i, fs, :], 1, 1)
+            ga += dot(cot_ref[:, i * dz : (i + 1) * dz], w2(i)[fs, :], 1, 1)
         ga = ga.astype(bf16).astype(f32)
         u2 = u * u
         t = jnp.tanh(C0 * (u + C1 * (u2 * u)))
@@ -403,8 +926,8 @@
     act, gh = act_s[...], gh_s[...]
     cot_loc = cot_ref[:, local]
     normed_loc = normed_ref[:, local]
-    part_ref[...] = part_in[...] + dot(act, w2_ref[z], 1, 0)
-    gpart_ref[...] = gpart_in[...] + dot(gh, w1_ref[local, :], 1, 1)
+    part_ref[...] = part_in[...] + dot(act, w2(z)[...], 1, 0)
+    gpart_ref[...] = gpart_in[...] + dot(gh, w1(z)[...], 1, 1)
 
     @pl.when(s == 0)
     def _():
@@ -425,7 +948,7 @@
     return pl.BlockSpec(s, lambda i: (0,) * len(s))
 
 
-def shards(hidden_in, cotangent, segment_ids, w_qkv, b_qkv, w_fc1, b_fc1, w_dense, w_fc2, out_bias, ln_gain, ln_shift):
+def shards_apart(hidden_in, cotangent, segment_ids, w_qkv, b_qkv, w_fc1, b_fc1, w_dense, w_fc2, out_bias, ln_gain, ln_shift):
     nd, nr, nc = lax.axis_size("dp"), lax.axis_size("row"), lax.axis_size("col")
     x, z = lax.axis_index("dp"), lax.axis_index("col")
     seq_len = segment_ids.shape[1]
@@ -439,78 +962,96 @@
 
     both = jnp.stack([hidden_in, cotangent])
     dma = pltpu.SemaphoreType.DMA
-    pair = pl.pallas_call(
+    wq = half(w_qkv, aw, 2).reshape(dz, 3 * aw)
+    bq = half(b_qkv, aw, 1).astype(f32).reshape(1, 3 * aw)
+    b1 = half(b_fc1, fw, 0).astype(f32).reshape(1, fw)
+    nchunk = 2
+    fc = fw // nchunk
+    chunks = []
+    for i in range(nchunk):
+        w1 = lax.dynamic_slice_in_dim(w_fc1, x * fw + i * fc, fc, 1)
+        w2 = lax.dynamic_slice_in_dim(w_fc2, x * fw + i * fc, fc, 0)
+        if fc == dz:
+            chunks.append([lax.all_gather(jnp.stack([w1, w2]), "col", axis=0)])
+        else:
+            chunks.append([lax.all_gather(w1, "col", axis=0), lax.all_gather(w2, "col", axis=0)])
+    sw = max(dz, seq_len)
+    line = lambda a: jnp.pad(a.astype(f32), ((0, 0), (0, sw - a.shape[1])))
+    small = jnp.concatenate(
+        [line(ln_gain[None]), line(ln_shift[None]), line(segment_ids), jnp.zeros((5, sw), f32)], axis=0
+    )
+    hbm = pl.BlockSpec(memory_space=pl.ANY)
+    ns = nd * nc
+    pair, wq_all, wd_all, small_all = pl.pallas_call(
         gather_kernel,
-        in_specs=[pl.BlockSpec(memory_space=pl.ANY)],
-        out_specs=pl.BlockSpec(memory_space=pl.ANY),
-        out_shape=shape((2, T, D), bf16),
+        in_specs=[hbm] * 4,
+        out_specs=[hbm] * 4,
+        out_shape=[shape((2, T, D), bf16), shape((D, 3 * aw), bf16), shape((nc, aw, dz), bf16), shape((ns, 8, sw), f32)],
         scratch_shapes=[
-            dma, dma((2, nc)), dma((nc,)), dma((2, nc)), dma((2, nc)), dma((2, nc)), dma((2, nc)), dma((4, nc)), dma((4, nc)),
+            dma((4,)), dma((2, nc)), dma((nc,)), dma((2, nc)), dma((2, nc)), dma((2, nc)), dma((2, nc)), dma((4, nc)), dma((4, nc)),
+            dma((2, 2, nc)), dma((2, nc)), dma((ns - 1,)), dma((ns - 1,)),
         ],
         compiler_params=pltpu.CompilerParams(collective_id=0, has_side_effects=True),
         name="gather",
-    )(both)
-    segs = lax.all_gather(segment_ids, ("dp", "col"), axis=0, tiled=True)
-    gain_all, shift_all = lax.all_gather(jnp.stack([ln_gain, ln_shift]), "col", axis=1, tiled=True).astype(f32)
-
-    wq = half(w_qkv, aw, 2).reshape(dz, 3 * aw)
-    wd = half(w_dense, aw, 0)
-    w1 = half(w_fc1, fw, 1)
-    w2 = half(w_fc2, fw, 0)
-    bq = half(b_qkv, aw, 1).astype(f32).reshape(1, 3 * aw)
-    b1 = half(b_fc1, fw, 0).astype(f32).reshape(1, fw)
-    wq_all = lax.all_gather(wq, "col", axis=0, tiled=True)
-    wd_all = lax.all_gather(wd, "col", axis=0)
-    nchunk = 2
-    fc = fw // nchunk
-    w1_all = [lax.all_gather(w1[:, i * fc : (i + 1) * fc], "col", axis=0, tiled=True) for i in range(nchunk)]
-    w2_all = [lax.all_gather(w2[i * fc : (i + 1) * fc], "col", axis=0) for i in range(nchunk)]
-
-    nb = min(256, seq_len)
-    normed, stat = pl.pallas_call(
-        norm_kernel,
-        grid=(T // nb,),
-        in_specs=[pl.BlockSpec((1, nb, D), lambda i: (0, i, 0)), whole((1, D)), whole((1, D))],
-        out_specs=[pl.BlockSpec((nb, D), lambda i: (i, 0)), pl.BlockSpec((nb, 128), lambda i: (i, 0))],
-        out_shape=[shape((T, D), bf16), shape((T, 128), f32)],
-        name="norm",
-    )(pair, gain_all.reshape(1, D), shift_all.reshape(1, D))
-
-    tables = rotary_tables(segs)
-    cot_blk = lambda n: pl.BlockSpec((None, n, D), lambda i: (1, i, 0))
+    )(both, wq, w_dense, small)
+
     blk = lambda n, w: pl.BlockSpec((n, w), lambda i: (i, 0))
-    seq_blk = lambda a, b: pl.BlockSpec((1, a, b), lambda i: (i, 0, 0))
-    part, gpart, dwq, dwd, dbq = pl.pallas_call(
+    normed, stat, part, gpart, dwq, dwd, dbq, dob = pl.pallas_call(
         attn_kernel,
         grid=(nseq,),
         in_specs=[
-            blk(seq_len, D), cot_blk(seq_len), whole((D, 3 * aw)), whole((nc, aw, dz)), whole((1, 3 * aw)),
-            seq_blk(seq_len, 128), seq_blk(seq_len, 128), seq_blk(seq_len, 128), seq_blk(1, seq_len), seq_blk(seq_len, 1),
+            pl.BlockSpec((2, seq_len, D), lambda i: (0, i, 0)), whole((D, 3 * aw)), whole((nc, aw, dz)), whole((1, 3 * aw)),
+            whole((ns, 8, sw)),
         ],
-        out_specs=[blk(seq_len, dz), blk(seq_len, dz), whole((dz, 3 * aw)), whole((aw, dz)), whole((1, 3 * aw))],
+        out_specs=[
+            blk(seq_len, D), blk(seq_len, 128), blk(seq_len, dz), blk(seq_len, dz),
+            whole((dz, 3 * aw)), whole((aw, dz)), whole((1, 3 * aw)), whole((1, dz)),
+        ],
         out_shape=[
-            shape((T, dz), f32), shape((T, dz), f32), shape((dz, 3 * aw), f32), shape((aw, dz), f32), shape((1, 3 * aw), f32),
+            shape((T, D), bf16), shape((T, 128), f32), shape((T, dz), f32), shape((T, dz), f32),
+            shape((dz, 3 * aw), f32), shape((aw, dz), f32), shape((1, 3 * aw), f32), shape((1, dz), f32),
         ],
         name="attn",
-    )(normed, pair, wq_all, wd_all, bq, *tables, segs[:, None, :], segs[:, :, None])
+    )(pair, wq_all, wd_all, bq, small_all)
+    swap = lambda a: lax.ppermute(a, "dp", [(i, nd - 1 - i) for i in range(nd)])
+
+    def join(a, axis):
+        b = swap(a)
+        return jnp.concatenate([jnp.where(x == 0, a, b), jnp.where(x == 0, b, a)], axis=axis)
+
+    def put(into, a, i, axis):
+        at = lambda who: [0] * axis + [who * fw + i * fc] + [0] * (1 - axis)
+        into = lax.dynamic_update_slice(into, a, at(x))
+        return lax.dynamic_update_slice(into, swap(a), at(1 - x))
+
+    g_qkv = join(dwq.reshape(dz, 3, aw), 2)
+    g_bq = join(dbq.reshape(3, aw), 1)
+    g_dense = join(dwd, 0)
+    g_fc1 = jnp.zeros((dz, nd * fw), f32)
+    g_fc2 = jnp.zeros((nd * fw, dz), f32)
+    g_b1 = jnp.zeros((1, nd * fw), f32)
 
     tb = 512
-    dw1s, dw2s, db1s = [], [], []
+    cot_blk = lambda n: pl.BlockSpec((None, n, D), lambda i: (1, i, 0))
+    if len(chunks[0]) == 1:
+        w_specs = [whole((nc, 2, dz, fc))]
+    else:
+        w_specs = [whole((nc, dz, fc)), whole((nc, fc, dz))]
     for i in range(nchunk):
         part, gpart, a, b, c = pl.pallas_call(
-            mlp_kernel,
+            functools.partial(mlp_kernel, len(chunks[i]) == 1),
             grid=(T // tb,),
             in_specs=[
-                blk(tb, D), cot_blk(tb), whole((D, fc)), whole((nc, fc, dz)), whole((1, fc)), blk(tb, dz), blk(tb, dz),
+                blk(tb, D), cot_blk(tb), *w_specs, whole((1, fc)), blk(tb, dz), blk(tb, dz),
             ],
             out_specs=[blk(tb, dz), blk(tb, dz), whole((dz, fc)), whole((fc, dz)), whole((1, fc))],
             out_shape=[shape((T, dz), f32), shape((T, dz), f32), shape((dz, fc), f32), shape((fc, dz), f32), shape((1, fc), f32)],
             scratch_shapes=[pltpu.VMEM((tb, fc), bf16), pltpu.VMEM((tb, fc), bf16)],
             name="mlp",
-        )(normed, pair, w1_all[i], w2_all[i], b1[:, i * fc : (i + 1) * fc], part, gpart)
-        dw1s.append(a)
-        dw2s.append(b)
-        db1s.append(c)
+        )(normed, pair, *chunks[i], b1[:, i * fc : (i + 1) * fc], part, gpart)
+        g_fc1 = put(g_fc1, a, i, 1)
+        g_fc2 = put(g_fc2, b, i, 0)
+        g_b1 = put(g_b1, c, i, 1)
 
     me = lax.axis_index(("dp", "row"))
     stat_l = lax.dynamic_slice_in_dim(stat, me * nloc, nloc, 0)
@@ -530,23 +1071,68 @@
         compiler_params=pltpu.CompilerParams(collective_id=1, has_side_effects=True),
         name="tail",
     )(part, gpart, both, stat_l, ln_gain.astype(f32).reshape(1, dz), out_bias.astype(f32).reshape(1, dz))
-    cot_loc = lax.dynamic_slice(pair, (1, 0, z * dz), (1, T, dz))[0]
-    d_ob = jnp.sum(cot_loc.astype(f32), axis=0)
-
-    ag = lambda a, axis: lax.all_gather(a, "dp", axis=axis, tiled=True)
-    return (
-        output,
-        grad_input,
-        ag(dwq.reshape(dz, 3, aw), 2),
-        ag(dbq.reshape(3, aw), 1),
-        ag(jnp.concatenate(dw1s, axis=1), 1),
-        ag(jnp.concatenate(db1s, axis=1)[0], 0),
-        ag(dwd, 0),
-        ag(jnp.concatenate(dw2s, axis=0), 0),
-        d_ob,
-        vec[0],
-        vec[1],
+    return (output, grad_input, g_qkv, g_bq, g_fc1, g_b1[0], g_dense, g_fc2, dob[0], vec[0], vec[1])
+
+
+def shards_whole(hidden_in, cotangent, segment_ids, w_qkv, b_qkv, w_fc1, b_fc1, w_dense, w_fc2, out_bias, ln_gain, ln_shift):
+    nd, nr, nc = lax.axis_size("dp"), lax.axis_size("row"), lax.axis_size("col")
+    x = lax.axis_index("dp")
+    n, dz = hidden_in.shape
+    seq = segment_ids.shape[1]
+    D, T = dz * nc, n * nd * nr
+    aw, fw = w_qkv.shape[2] // nd, w_fc1.shape[1] // nd
+    nj = 4
+    fc = fw // nj
+    ns, npl = nd * nc, nd * nr
+    half = lambda w, size, axis: lax.dynamic_slice_in_dim(w, x * size, size, axis)
+    wq = half(w_qkv, aw, 2).reshape(dz, 3 * aw)
+    bq = half(b_qkv, aw, 1).astype(f32).reshape(1, 3 * aw)
+    b1 = half(b_fc1, fw, 0).astype(f32).reshape(nj, 1, fc)
+    sw = max(dz, seq)
+    line = lambda a: jnp.pad(a.astype(f32), ((0, 0), (0, sw - a.shape[1])))
+    small = jnp.concatenate([line(ln_gain[None]), line(ln_shift[None]), line(segment_ids), jnp.zeros((5, sw), f32)], axis=0)
+    hbm, vmem = pl.BlockSpec(memory_space=pl.ANY), pl.BlockSpec(memory_space=pltpu.VMEM)
+    dma = pltpu.SemaphoreType.DMA
+    v = pltpu.VMEM
+    nk = 4 + 2 * nj
+    gw = max(3 * aw, fc)
+    out, gin, vec, gb, gq, gd, g1, g2 = pl.pallas_call(
+        layer_kernel,
+        in_specs=[vmem, hbm, hbm, hbm, hbm, vmem, vmem, vmem, vmem, vmem],
+        out_specs=[vmem] * 4 + [hbm] * 4,
+        out_shape=[
+            shape((n, dz), bf16), shape((n, dz), f32), shape((8, dz), f32), shape((nd, nj + 1, 8, gw), f32),
+            shape((3, dz, nd * aw), f32), shape((nd * aw, dz), f32), shape((dz, nd * fw), f32), shape((nd * fw, dz), f32),
+        ],
+        scratch_shapes=[
+            v((2, T, D), bf16), v((nc, dz, 3 * aw), bf16), v((nc, aw, dz), bf16),
+            v((nj, nc, dz, fc), bf16), v((nj, nc, fc, dz), bf16),
+            v((T, dz), f32), v((T, dz), f32), v((dz, 3 * aw), f32), v((aw, dz), f32), v((nj, dz, fc), f32), v((nj, fc, dz), f32),
+            v((T, 128), f32), v((ns, 8, sw), f32), v((2, 4, n, dz), f32), v((2, 2, n, dz), f32), v((2, n, dz), f32),
+            v((nc, 8, n), f32), v((npl, 8, dz), f32),
+            dma((4 + 2 * nj,)), dma((2, nc)), dma((nc,)), dma((2, nc)), dma((2, nc)), dma((2, nc)), dma((2, nc)), dma((4, nc)), dma((4, nc)),
+            dma((2, 2, nc)), dma((2, nc)), dma((2, 2, nj, nc)), dma((2, nj, nc)), dma((ns - 1,)), dma((ns - 1,)),
+            dma((nk,)), dma((nk,)), dma((nk,)), dma, dma,
+            dma((2, 4)), dma((2, 4)), dma((2, 2)), dma((2, 2)), dma((2,)), dma((2,)),
+            dma((nc - 1,)), dma((nc - 1,)), dma((npl - 1,)), dma((npl - 1,)),
+        ],
+        compiler_params=pltpu.CompilerParams(collective_id=0, has_side_effects=True, vmem_limit_bytes=67043328),
+        name="layer",
+    )(
+        jnp.stack([hidden_in, cotangent]), wq, w_dense, w_fc1, w_fc2, bq, b1, small,
+        ln_gain.astype(f32).reshape(1, dz), out_bias.astype(f32).reshape(1, dz),
     )
+    g_bq = gb[:, 0, 0, : 3 * aw].reshape(nd, 3, aw).transpose(1, 0, 2).reshape(3, nd * aw)
+    g_b1 = gb[:, 1:, 0, :fc].reshape(nd * fw)
+    return (out, gin, gq.transpose(1, 0, 2), g_bq, g1, g_b1, gd, g2, vec[2], vec[0], vec[1])
+
+
+def shards(*args):
+    n, dz = args[0].shape
+    nd, nr, nc = lax.axis_size("dp"), lax.axis_size("row"), lax.axis_size("col")
+    tokens = n * nd * nr * dz * nc
+    fits = nc == 4 and nd == 2 and nr == 4 and args[2].shape[1] == n and tokens <= 1 << 22
+    return (shards_whole if fits else shards_apart)(*args)
 
 
 def solution(mesh):

time: 534 us -> 366 us (0.69)
  waiting for transfers between devices: 120 us -> 0 us
  Pallas kernels: 289 us -> 335 us
  blocking collectives: 44.7 us -> 0 us
  local copies, waits for them, and re-layouts: 48.1 us -> 21.6 us
  between operations: 14.5 us -> 0.69 us
  other arithmetic: 15.5 us -> 7.81 us
    all_gather x10 -> x0, waiting for transfers between devices: 119 us -> none  [the longest x4 88.4 us: shards(): ag = lambda a, axis: lax.all_gather(a, 'dp', axis=axis, tiled=True)]
    pallas_call x6 -> x1, Pallas kernels: 289 us -> 335 us  [shards_whole(): pl.pallas_call(layer_kernel, in_specs=[vmem, hbm, hbm, hbm, hbm, vmem, vm...]
    all_gather x4 -> x0, blocking collectives: 44.7 us -> none  [the longest x1 23 us: shards(): segs = lax.all_gather(segment_ids, ('dp', 'col'), axis=0, tiled=True)]
    concatenate x3 -> x1, local copies, waits for them, and re-layouts: 12.8 us -> 0.07 us  [shards_whole(): jnp.concatenate([line(ln_gain[None]), line(ln_shift[None]), line(segment_...]
    sin x1 -> x0, other arithmetic: 5.51 us -> none  [rotary_tables(): cosine, sine = (jnp.cos(angles), jnp.sin(angles))]
    unnamed x53 -> x16, local copies, waits for them, and re-layouts: 17.7 us -> 14.8 us
  transfers between devices with their start and end apart: 10 -> 0, of which waited for: 3 -> 0; matrix products, arithmetic and copies ran while one was open for 9% -> 0% of each run, Pallas kernels for 54% -> 0%
where the time goes in v2:
time: 366 us; the launch traced here: 365 us
  Pallas kernels  335 us (92%)
  local copies, waits for them, and re-layouts  21.6 us (6%)
  other arithmetic  7.81 us (2%)
    pallas_call x1, Pallas kernels, shards_whole(): pl.pallas_call(layer_kernel, in_specs=[vmem, hbm, hbm, hbm, hbm, vmem, vm...  335 us
    unnamed x16, local copies, waits for them, and re-layouts  14.8 us

profile of v2, /device:TPU:0, one launch (start us, length us, event | category | flops | bytes accessed | tf_op | source)
XLA Modules:
  0.0 365.3 jit_solution(11233217762642657127)
XLA Ops:
  0.7 0.1 pad.8.clone
  0.7 0.7 convert_element_type.25
  1.4 1.3 reshape.62
  2.7 0.7 convert_element_type.26
  3.4 0.0 copy-start.3
  3.4 0.7 convert_element_type.27
  4.0 1.3 dynamic-slice_convert_fusion
  5.3 0.7 convert_bitcast_fusion
  6.0 0.6 copy.28
  6.6 0.0 copy-done.3
  6.6 0.7 fusion.small_ref
  7.3 1.9 pad_maximum_fusion.both_ref
  9.1 1.2 constant_dynamic-slice_fusion
  10.3 0.3 copy.27
  10.6 1.2 copy.26.wq_ref
  11.8 335.3 %layer.1 = (bf16[256,512]{1,0:T(8,128)(2,1)}, f32[256,512]{1,0:T(8,128)}, f32[8,512]{1,0:T(8,128)}, f32[2,5,8,768]{3,2,1,0:T(8,128)}, f32[3,512,512]{2,1,0:T(8,1...) custom-call(bf16[2,256,512]{2,1,0:T(8,128)(2,1)} %pad_maximum_fusion.both_ref, ...), custom_call_target="tpu_custom_call" | custom-call | tf_op jit(solution)/shard_map/layer/pallas_call | solution.py:1099
  347.1 0.8 slice_reduce_fusion
  347.9 1.4 slice.16
  349.3 0.6 reshape_squeeze.6
  349.9 1.4 fusion.2
  351.4 1.7 copy.35
  353.0 1.9 copy.36
  354.9 0.0 copy-start.1
  354.9 4.0 %copy.37 = f32[512,3,512]{2,0,1:T(8,128)} copy(f32[512,3,512]{2,0,1:T(8,128)} %bitcast.19) | data formatting | bytes 6291456
  358.9 0.0 copy-done.1
  358.9 0.0 copy-start.2
  358.9 0.0 copy-start
  358.9 2.1 copy.38
  361.1 0.0 copy-done.2
  361.1 1.0 copy.39
  362.0 1.3 copy-done
  363.3 2.0 copy.40
  (1 shorter events, 0.0 us)
Async XLA Ops:
  3.4 3.2 copy-start.3
  354.9 4.0 %copy-start.1 = (f32[512,2048]{1,0:T(8,128)S(1)}, f32[512,2048]{1,0:T(8,128)}, u32[]{:S(2)}) copy-start(f32[512,2048]{1,0:T(8,128)} %get-tuple-element.45) | copy-start | bytes 12582916
  358.9 2.1 copy-start.2
  358.9 4.4 %copy-start = (f32[2048,512]{1,0:T(8,128)S(1)}, f32[2048,512]{1,0:T(8,128)}, u32[]{:S(2)}) copy-start(f32[2048,512]{1,0:T(8,128)} %get-tuple-element.48) | copy-start | bytes 12582916
